TPU v7x, 32 devices: a whole 2x2x4 slice. The times are simulated.
32 devices in a mesh: group: 4 (over y, core), dev: 8 (over z, x).
Axes of the slice: x: 2, y: 2, z: 4, core: 2. Of those that a mesh axis runs over, the one named last changes fastest.
Arguments:
- solution: float32 [4, 16, 16, 512], P('group', 'dev'), may hold values from -6 to 6
- residual: float32 [4, 16, 16, 512], P('group', 'dev'), may hold values from -6 to 6
- direction: float32 [4, 16, 16, 512], P('group', 'dev'), may hold values from -0.03 to 0.03
- geometry: bfloat16 [3, 4, 16, 16, 512], P(None, 'group', 'dev'), may hold values from 0.5 to 2
- mass: bfloat16 [4, 16, 16, 512], P('group', 'dev'), may hold values from 50 to 500
Outputs:
- solution_out: float32 [4, 16, 16, 512], P('group', 'dev')
- residual_out: float32 [4, 16, 16, 512], P('group', 'dev')
- direction_out: float32 [4, 16, 16, 512], P('group', 'dev')
All inputs are finite; a program needn't handle non-finite values.
Results may differ from a plain program's by a relative error of at most 0.0003.
Values sent between devices are 32-bit elements; how exact they have to be, the bound alone decides.
A program may use at most 64 MiB of HBM per device.

v0:
```python
import functools

import jax
import jax.numpy as jnp
import numpy as np
from jax import lax
from jax.experimental import pallas as pl
from jax.experimental.pallas import tpu as pltpu
from jax.sharding import PartitionSpec as P

NP = 8
LANES = 128
MESH = pl.DeviceIdType.MESH

lobatto_nodes = [
    -1.0,
    -0.8717401485096066,
    -0.5917001814331423,
    -0.2092992179024789,
    0.2092992179024789,
    0.5917001814331423,
    0.8717401485096066,
    1.0,
]


def derivative_table():
    nodes = np.array(lobatto_nodes)
    identity = np.eye(NP)
    offset = nodes[:, None] - nodes[None, :] + identity
    barycentric = 1.0 / np.prod(offset, axis=1)
    derivative = barycentric[None, :] / barycentric[:, None] / offset * (1.0 - identity)
    return derivative - identity * np.sum(derivative, axis=1)[:, None]


def split_table(table):
    table = np.asarray(table, np.float32)
    high = table.astype(jnp.bfloat16)
    low = (table - high.astype(np.float32)).astype(jnp.bfloat16)
    return high, low


def tables():
    d = derivative_table().astype(np.float32)
    along_j = np.kron(np.kron(np.eye(2), d), np.eye(NP))
    along_k = np.kron(np.eye(16), d)
    high, low = split_table(np.concatenate([along_j.T, along_k.T], axis=1))
    forward = np.concatenate([np.concatenate([high, high], 0), np.concatenate([low, low], 0)], 1)
    high, low = split_table(np.concatenate([along_j, along_k], axis=0))
    backward = np.concatenate([high, low], axis=1)
    high, low = split_table(np.concatenate([along_j * along_j, along_k * along_k], axis=0))
    squares = np.concatenate([high, low], axis=1)
    return np.concatenate([forward, backward, squares], axis=1)


def roll(x, shift):
    shift %= LANES
    return x if shift == 0 else pltpu.roll(x, shift, 1)


def lane_of(shape):
    return lax.broadcasted_iota(jnp.int32, shape, 1)


def along_i(table, blocks):
    low = lane_of(blocks[0].shape) < 64
    swapped = [roll(x, 64) for x in blocks]
    outs = []
    for b in range(4):
        total = None
        for c in range(4):
            same = jnp.where(low, float(table[2 * b, 2 * c]), float(table[2 * b + 1, 2 * c + 1]))
            other = jnp.where(low, float(table[2 * b, 2 * c + 1]), float(table[2 * b + 1, 2 * c]))
            term = same * blocks[c] + other * swapped[c]
            total = term if total is None else total + term
        outs.append(total)
    return outs


def weights_of(rows):
    lane = lane_of((rows, LANES))
    k, j = lane & 7, (lane >> 3) & 7
    half = lambda cond: jnp.where(cond, 0.5, 1.0)
    base = half((k == 0) | (k == 7)) * half((j == 0) | (j == 7))
    return [base * half(lane < 64), base, base, base * half(lane >= 64)]


def pack_i_face(x, side):
    h = x.shape[0] // 2
    top, bottom = x[:h], x[h:]
    low = lane_of(top.shape) < 64
    if side == 0:
        return jnp.where(low, top, roll(bottom, 64))
    return jnp.where(low, roll(top, 64), bottom)


def unpack_i_face(m, side):
    other = roll(m, 64)
    return jnp.concatenate([m, other] if side == 0 else [other, m], axis=0)


def pack_j_face(blocks, ez, side):
    half = ez // 2
    lane = lane_of((half, LANES))
    slot = (lane & 63) >> 3
    out = jnp.zeros((half, LANES), jnp.float32)
    for b in range(4):
        rows = blocks[b][:ez] if side == 0 else blocks[b][-ez:]
        for n in range(2):
            moved = roll(rows[n * half : (n + 1) * half], 8 * b + 32 * n - (0 if side == 0 else 56))
            out = jnp.where(slot == b + 4 * n, moved, out)
    return out


def unpack_j_face(m, b, shift):
    return jnp.concatenate([roll(m, shift - 8 * b), roll(m, shift - 8 * b - 32)], axis=0)


def join_j_faces(mine, before, after):
    lane = lane_of(mine.shape)
    first = (lane < 64) & ((lane & 31) < 8)
    last = (lane >= 64) & ((lane & 31) >= 24)
    return mine + jnp.where(first, roll(before, 40), jnp.where(last, roll(after, 88), 0.0))


def finish_assembly(blocks, ez, i_prev, i_next, j_prev, j_next):
    rows = blocks[0].shape[0]
    lane = lane_of((rows, LANES))
    low = lane < 64
    j, k = (lane >> 3) & 7, lane & 7
    blocks = list(blocks)
    blocks[0] = blocks[0] + jnp.where(low, unpack_i_face(i_prev, 0), 0.0)
    blocks[3] = blocks[3] + jnp.where(low, 0.0, unpack_i_face(i_next, 1))
    outs = []
    for b, x in enumerate(blocks):
        after, before = unpack_j_face(j_next, b, 56), unpack_j_face(j_prev, b, 0)
        if rows > ez:
            after = jnp.concatenate([roll(x[ez:], 56), after], axis=0)
            before = jnp.concatenate([before, roll(x[:-ez], -56)], axis=0)
        x = x + jnp.where(j == 7, after, jnp.where(j == 0, before, 0.0))
        up, down = roll(x, 7), roll(x, -7)
        after = [pltpu.roll(up[e : e + ez], ez - 1, 0) for e in range(0, rows, ez)]
        before = [pltpu.roll(down[e : e + ez], 1, 0) for e in range(0, rows, ez)]
        after, before = jnp.concatenate(after, 0), jnp.concatenate(before, 0)
        outs.append(x + jnp.where(k == 7, after, jnp.where(k == 0, before, 0.0)))
    return outs


def halves(x):
    high = x.astype(jnp.bfloat16)
    return high, (x - high.astype(jnp.float32)).astype(jnp.bfloat16)


def dot(left, right):
    return jnp.dot(left, right, preferred_element_type=jnp.float32)


def stack(blocks):
    return jnp.concatenate(blocks, axis=0)


def total_of(blocks):
    x = blocks[0] + blocks[1] + (blocks[2] + blocks[3])
    return jnp.sum(jnp.sum(x, axis=0, keepdims=True), axis=1, keepdims=True)


def kernel(
    ng, nd, ez,
    sol_h, res_h, dir_h, geo_h, mass_h, tab_h,
    sol_o, res_o, dir_o,
    sol_v, res_v, dir_v, geo_v, mass_v, tab_v,
    i_out, i_in, j_out, j_in, part, parts,
    load_sem, send_sem, recv_sem, part_send, part_recv,
):
    me_g, me_d = lax.axis_index("group"), lax.axis_index("dev")

    def at(a, b):
        return (lax.rem(me_g + (a + ng), ng), lax.rem(me_d + (b + nd), nd))

    others = [(a, b) for a in range(ng) for b in range(nd) if (a, b) != (0, 0)]
    others.sort(key=lambda t: (min(t[1], nd - t[1]) != 1, min(t[0], ng - t[0]) > 1))
    barrier = pltpu.get_barrier_semaphore()
    for a, b in others:
        pl.semaphore_signal(barrier, inc=1, device_id=at(a, b), device_id_type=MESH)

    pairs = ((dir_h, dir_v), (geo_h, geo_v), (mass_h, mass_v), (tab_h, tab_v), (res_h, res_v), (sol_h, sol_v))
    loads = [pltpu.make_async_copy(h, v, load_sem.at[n]) for n, (h, v) in enumerate(pairs)]
    for load in loads:
        load.start()

    rows = dir_v.shape[0]
    weights = weights_of(rows)
    cut = [slice(LANES * b, LANES * b + LANES) for b in range(4)]

    def exchange(phase, blocks, started=True):
        made = []

        def give(src, dst, target):
            n = len(made)
            made.append(
                pltpu.make_async_remote_copy(
                    src_ref=src, dst_ref=dst,
                    send_sem=send_sem.at[phase, n], recv_sem=recv_sem.at[phase, n],
                    device_id=target, device_id_type=MESH,
                )
            )
            if started:
                made[-1].start()

        for side, step in ((0, -1), (1, 1)):
            i_out[phase, side] = pack_i_face(blocks[3 * side], side)
            give(i_out.at[phase, side], i_in.at[phase, side], at(step, 0))
        for side, step in ((1, 1), (0, -1)):
            j_out[phase, side] = pack_j_face(blocks, ez, side)
            for turn, a in ((0, -1), (2, 1), (1, 0)):
                give(j_out.at[phase, side], j_in.at[phase, side, turn], at(a, step))
        return made

    def assembled(phase, blocks):
        j_prev = join_j_faces(j_in[phase, 1, 1], j_in[phase, 1, 2], j_in[phase, 1, 0])
        j_next = join_j_faces(j_in[phase, 0, 1], j_in[phase, 0, 2], j_in[phase, 0, 0])
        return finish_assembly(blocks, ez, i_in[phase, 1], i_in[phase, 0], j_prev, j_next)

    d = derivative_table().astype(np.float32)
    loads[0].wait()
    weighted = [weights[b] * dir_v[:, cut[b]] for b in range(4)]
    first = exchange(0, weighted, started=False)
    pl.semaphore_wait(barrier, len(others))
    for copy in first:
        copy.start()
    for load in loads[1:4]:
        load.wait()
    geo_rows = stack([jnp.concatenate([geo_v[1, :, c], geo_v[2, :, c]], axis=1) for c in cut])
    squared = dot(geo_rows, tab_v[:, 768:1024])
    squared = squared[:, :LANES] + squared[:, LANES:]
    geo = [[geo_v[c, :, cut[b]].astype(jnp.float32) for b in range(4)] for c in range(3)]
    mass = [mass_v[:, c].astype(jnp.float32) for c in cut]
    diag = along_i((d * d).T, geo[0])
    diag = [diag[b] + squared[rows * b : rows * b + rows] + mass[b] for b in range(4)]
    side_copies = exchange(1, diag)
    loads[4].wait()
    loads[5].wait()
    for copy in first:
        copy.wait_recv()
    smooth = assembled(0, weighted)

    high, low = halves(stack(smooth))
    grads = dot(jnp.concatenate([high, low], axis=1), tab_v[:, :512])
    grads = grads[:, :256] + grads[:, 256:]
    grad_i = along_i(d, smooth)
    flux_i = [geo[0][b] * grad_i[b] for b in range(4)]
    flux = jnp.concatenate(
        [stack(geo[1]) * grads[:, :LANES], stack(geo[2]) * grads[:, LANES:]], axis=1
    )
    high, low = halves(flux)
    back = dot(jnp.concatenate([high, low], axis=0), tab_v[:, 512:768])
    back = back[: 4 * rows] + back[4 * rows :]
    back = back[:, :LANES] + back[:, LANES:]
    local = along_i(d.T, flux_i)
    local = [local[b] + back[rows * b : rows * b + rows] + mass[b] * smooth[b] for b in range(4)]

    second = exchange(2, local)
    for copy in side_copies:
        copy.wait_recv()
    inverse = [1.0 / x for x in assembled(1, diag)]
    residual = [res_v[:, c] for c in cut]
    scaled = [residual[b] * inverse[b] for b in range(4)]
    norm_now = total_of([weights[b] * residual[b] * scaled[b] for b in range(4)])
    curvature = total_of([smooth[b] * local[b] for b in range(4)])
    for copy in second:
        copy.wait_recv()
    applied = assembled(2, local)
    shared = [weights[b] * applied[b] for b in range(4)]
    cross = total_of([shared[b] * scaled[b] for b in range(4)])
    quad = total_of([shared[b] * applied[b] * inverse[b] for b in range(4)])

    lane = lane_of((1, LANES))
    mine = jnp.where(
        lane < 32, norm_now, jnp.where(lane < 64, curvature, jnp.where(lane < 96, cross, quad))
    )
    part[0] = mine
    for n, (a, b) in enumerate(others):
        pltpu.make_async_remote_copy(
            src_ref=part.at[0], dst_ref=parts.at[n],
            send_sem=part_send, recv_sem=part_recv,
            device_id=at(a, b), device_id_type=MESH,
        ).start()
    pltpu.make_async_copy(parts, parts, part_recv).wait()
    everyone = mine + jnp.sum(parts[...], axis=0)
    norm_now, curvature, cross, quad = (everyone[:, 32 * n : 32 * n + 1] for n in range(4))
    step = norm_now / curvature
    norm_next = norm_now - 2.0 * step * cross + step * step * quad
    ratio = norm_next / norm_now
    for b, c in enumerate(cut):
        sol_o[:, c] = sol_v[:, c] + step * smooth[b]
        out = residual[b] - step * applied[b]
        res_o[:, c] = out
        dir_o[:, c] = out * inverse[b] + ratio * smooth[b]
    for copy in first + side_copies + second:
        copy.wait_send()
    pltpu.make_async_copy(parts, parts, part_send).wait()


def deliver(*refs):
    copies = [pltpu.make_async_copy(refs[n], refs[3 + n], refs[6].at[n]) for n in range(3)]
    for copy in copies:
        copy.start()
    for copy in copies:
        copy.wait()


def on_device(solution, residual, direction, geometry, mass):
    dims = solution.shape
    ng, nd = lax.axis_size("group"), lax.axis_size("dev")
    ez, points = dims[2], dims[3]
    rows = dims[0] * dims[1] * ez
    flat = (rows, points)
    f32, bf16 = jnp.float32, jnp.bfloat16
    table = jnp.asarray(tables())
    h = rows // 2
    outs = pl.pallas_call(
        functools.partial(kernel, ng, nd, ez),
        out_shape=[pltpu.VMEM(flat, f32)] * 3,
        in_specs=[pl.BlockSpec(memory_space=pltpu.HBM)] * 6,
        out_specs=[pl.BlockSpec(memory_space=pltpu.VMEM)] * 3,
        scratch_shapes=[
            pltpu.VMEM(flat, f32),
            pltpu.VMEM(flat, f32),
            pltpu.VMEM(flat, f32),
            pltpu.VMEM((3,) + flat, bf16),
            pltpu.VMEM(flat, bf16),
            pltpu.VMEM(table.shape, bf16),
            pltpu.VMEM((3, 2, h, LANES), f32),
            pltpu.VMEM((3, 2, h, LANES), f32),
            pltpu.VMEM((3, 2, ez // 2, LANES), f32),
            pltpu.VMEM((3, 2, 3, ez // 2, LANES), f32),
            pltpu.VMEM((1, 1, LANES), f32),
            pltpu.VMEM((ng * nd - 1, 1, LANES), f32),
            pltpu.SemaphoreType.DMA((6,)),
            pltpu.SemaphoreType.DMA((3, 8)),
            pltpu.SemaphoreType.DMA((3, 8)),
            pltpu.SemaphoreType.DMA,
            pltpu.SemaphoreType.DMA,
        ],
        compiler_params=pltpu.CompilerParams(collective_id=0, has_side_effects=True, vmem_limit_bytes=8 << 20),
    )(
        pltpu.with_memory_space_constraint(solution.reshape(flat), pltpu.HBM),
        pltpu.with_memory_space_constraint(residual.reshape(flat), pltpu.HBM),
        pltpu.with_memory_space_constraint(direction.reshape(flat), pltpu.HBM),
        pltpu.with_memory_space_constraint(geometry.reshape((3,) + flat), pltpu.HBM),
        pltpu.with_memory_space_constraint(mass.reshape(flat), pltpu.HBM),
        pltpu.with_memory_space_constraint(table, pltpu.HBM),
    )
    outs = pl.pallas_call(
        deliver,
        out_shape=[jax.ShapeDtypeStruct(flat, f32)] * 3,
        in_specs=[pl.BlockSpec(memory_space=pl.ANY)] * 3,
        out_specs=[pl.BlockSpec(memory_space=pltpu.HBM)] * 3,
        scratch_shapes=[pltpu.SemaphoreType.DMA((3,))],
        compiler_params=pltpu.CompilerParams(vmem_limit_bytes=8 << 20),
    )(*outs)
    return tuple(x.reshape(dims) for x in outs)


def solution(mesh):
    spec = P("group", "dev", None, None)
    return jax.shard_map(
        on_device,
        mesh=mesh,
        in_specs=(spec, spec, spec, P(None, "group", "dev", None, None), spec),
        out_specs=(spec, spec, spec),
        check_vma=False,
    )
```

profile of v0, /device:TPU:0, one launch (start us, length us, event | category | flops | bytes accessed | tf_op | source)
XLA Modules:
  0.0 20.9 jit_solution(12734376420679152910)
XLA Ops:
  0.6 19.5 %shard_map.85 = (f32[32,512]{1,0:T(8,128)S(1)}, f32[32,512]{1,0:T(8,128)S(1)}, f32[32,512]{1,0:T(8,128)S(1)}) custom-call(f32[32,512]{1,0:T(8,128)} %bitcast.9, f32[32,512]{1,0:T(8,128)} %bitcast.10, f32[32,512]{1,0:T(8,128)} %bitcast.11, bf16[3,32,512]{2,1,0:T(8,128)(2,1)} %bitcast.8, bf16[32,512]{1,0:T(8,128)(2,1)} %bitcast.12, ...), custom_call_target="tpu_custom_call" | custom-call | tf_op jit(solution)/shard_map/pallas_call | solution.py:321
  20.2 0.7 %shard_map.86 = (f32[32,512]{1,0:T(8,128)}, f32[32,512]{1,0:T(8,128)}, f32[32,512]{1,0:T(8,128)}) custom-call(f32[32,512]{1,0:T(8,128)S(1)} %get-tuple-element.9.refs_0_, f32[32,512]{1,0:T(8,128)S(1)} %get-tuple-element.10.refs_1_, f32[32,512]{1,0:T(8,128)S(1)} %get-tuple-element.11.refs_2_), custom_call_target="tpu_custom_call" | custom-call | tf_op jit(solution)/shard_map/pallas_call | solution.py:354
where the time goes:
time: 21 us; the launch traced here: 20.9 us
  Pallas kernels  20.2 us (96%)
  between operations  0.64 us (3%)
    pallas_call x1, Pallas kernels, on_device(): pl.pallas_call(functools.partial(kernel, ng, nd, ez), out_shape=[pltpu.VM...  19.5 us
    pallas_call x1, Pallas kernels, on_device(): pl.pallas_call(deliver, out_shape=[jax.ShapeDtypeStruct(flat, f32)] * 3,...  0.7 us

commit v1 on v0

--- a/solution.py
+++ b/solution.py
@@ -167,9 +167,9 @@
 def kernel(
     ng, nd, ez,
     sol_h, res_h, dir_h, geo_h, mass_h, tab_h,
-    sol_o, res_o, dir_o,
+    outs,
     sol_v, res_v, dir_v, geo_v, mass_v, tab_v,
-    i_out, i_in, j_out, j_in, part, parts,
+    face_out, face_in, part, parts,
     load_sem, send_sem, recv_sem, part_send, part_recv,
 ):
     me_g, me_d = lax.axis_index("group"), lax.axis_index("dev")
@@ -179,16 +179,38 @@
 
     others = [(a, b) for a in range(ng) for b in range(nd) if (a, b) != (0, 0)]
     others.sort(key=lambda t: (min(t[1], nd - t[1]) != 1, min(t[0], ng - t[0]) > 1))
+
+    pairs = ((dir_h, dir_v), (geo_h, geo_v), (mass_h, mass_v), (tab_h, tab_v), (res_h, res_v), (sol_h, sol_v))
+    loads = [pltpu.make_async_copy(h, v, load_sem.at[n]) for n, (h, v) in enumerate(pairs)]
+    loads[0].start()
     barrier = pltpu.get_barrier_semaphore()
     for a, b in others:
         pl.semaphore_signal(barrier, inc=1, device_id=at(a, b), device_id_type=MESH)
 
-    pairs = ((dir_h, dir_v), (geo_h, geo_v), (mass_h, mass_v), (tab_h, tab_v), (res_h, res_v), (sol_h, sol_v))
-    loads = [pltpu.make_async_copy(h, v, load_sem.at[n]) for n, (h, v) in enumerate(pairs)]
-    for load in loads:
+    for load in loads[1:]:
         load.start()
 
     rows = dir_v.shape[0]
+    h, q = rows // 2, ez // 2
+
+    def window(ref, phase, start, size):
+        return ref.at[phase, pl.ds(start, size)]
+
+    def i_out(phase, side):
+        return window(face_out, phase, h * side, h)
+
+    def i_in(phase, side):
+        return window(face_in, phase, h * side, h)
+
+    def j_out(phase, side):
+        return window(face_out, phase, 2 * h + q * side, q)
+
+    def j_in(phase, side, turn):
+        return window(face_in, phase, 2 * h + q * (3 * side + turn), q)
+
+    def all_of(phase, sem):
+        pltpu.make_async_copy(face_in.at[phase], face_in.at[phase], sem.at[phase]).wait()
+
     weights = weights_of(rows)
     cut = [slice(LANES * b, LANES * b + LANES) for b in range(4)]
 
@@ -196,11 +218,10 @@
         made = []
 
         def give(src, dst, target):
-            n = len(made)
             made.append(
                 pltpu.make_async_remote_copy(
                     src_ref=src, dst_ref=dst,
-                    send_sem=send_sem.at[phase, n], recv_sem=recv_sem.at[phase, n],
+                    send_sem=send_sem.at[phase], recv_sem=recv_sem.at[phase],
                     device_id=target, device_id_type=MESH,
                 )
             )
@@ -208,18 +229,18 @@
                 made[-1].start()
 
         for side, step in ((0, -1), (1, 1)):
-            i_out[phase, side] = pack_i_face(blocks[3 * side], side)
-            give(i_out.at[phase, side], i_in.at[phase, side], at(step, 0))
+            i_out(phase, side)[...] = pack_i_face(blocks[3 * side], side)
+            give(i_out(phase, side), i_in(phase, side), at(step, 0))
         for side, step in ((1, 1), (0, -1)):
-            j_out[phase, side] = pack_j_face(blocks, ez, side)
+            j_out(phase, side)[...] = pack_j_face(blocks, ez, side)
             for turn, a in ((0, -1), (2, 1), (1, 0)):
-                give(j_out.at[phase, side], j_in.at[phase, side, turn], at(a, step))
+                give(j_out(phase, side), j_in(phase, side, turn), at(a, step))
         return made
 
     def assembled(phase, blocks):
-        j_prev = join_j_faces(j_in[phase, 1, 1], j_in[phase, 1, 2], j_in[phase, 1, 0])
-        j_next = join_j_faces(j_in[phase, 0, 1], j_in[phase, 0, 2], j_in[phase, 0, 0])
-        return finish_assembly(blocks, ez, i_in[phase, 1], i_in[phase, 0], j_prev, j_next)
+        j_prev = join_j_faces(*(j_in(phase, 1, turn)[...] for turn in (1, 2, 0)))
+        j_next = join_j_faces(*(j_in(phase, 0, turn)[...] for turn in (1, 2, 0)))
+        return finish_assembly(blocks, ez, i_in(phase, 1)[...], i_in(phase, 0)[...], j_prev, j_next)
 
     d = derivative_table().astype(np.float32)
     loads[0].wait()
@@ -237,11 +258,10 @@
     mass = [mass_v[:, c].astype(jnp.float32) for c in cut]
     diag = along_i((d * d).T, geo[0])
     diag = [diag[b] + squared[rows * b : rows * b + rows] + mass[b] for b in range(4)]
-    side_copies = exchange(1, diag)
+    exchange(1, diag)
     loads[4].wait()
     loads[5].wait()
-    for copy in first:
-        copy.wait_recv()
+    all_of(0, recv_sem)
     smooth = assembled(0, weighted)
 
     high, low = halves(stack(smooth))
@@ -259,16 +279,14 @@
     local = along_i(d.T, flux_i)
     local = [local[b] + back[rows * b : rows * b + rows] + mass[b] * smooth[b] for b in range(4)]
 
-    second = exchange(2, local)
-    for copy in side_copies:
-        copy.wait_recv()
+    exchange(2, local)
+    all_of(1, recv_sem)
     inverse = [1.0 / x for x in assembled(1, diag)]
     residual = [res_v[:, c] for c in cut]
     scaled = [residual[b] * inverse[b] for b in range(4)]
     norm_now = total_of([weights[b] * residual[b] * scaled[b] for b in range(4)])
     curvature = total_of([smooth[b] * local[b] for b in range(4)])
-    for copy in second:
-        copy.wait_recv()
+    all_of(2, recv_sem)
     applied = assembled(2, local)
     shared = [weights[b] * applied[b] for b in range(4)]
     cross = total_of([shared[b] * scaled[b] for b in range(4)])
@@ -279,7 +297,9 @@
         lane < 32, norm_now, jnp.where(lane < 64, curvature, jnp.where(lane < 96, cross, quad))
     )
     part[0] = mine
-    for n, (a, b) in enumerate(others):
+    order = sorted(range(len(others)), key=lambda n: (others[n][1] != 0, others[n][1] != 1))
+    for n in order:
+        a, b = others[n]
         pltpu.make_async_remote_copy(
             src_ref=part.at[0], dst_ref=parts.at[n],
             send_sem=part_send, recv_sem=part_recv,
@@ -292,21 +312,19 @@
     norm_next = norm_now - 2.0 * step * cross + step * step * quad
     ratio = norm_next / norm_now
     for b, c in enumerate(cut):
-        sol_o[:, c] = sol_v[:, c] + step * smooth[b]
+        outs[0, :, c] = sol_v[:, c] + step * smooth[b]
         out = residual[b] - step * applied[b]
-        res_o[:, c] = out
-        dir_o[:, c] = out * inverse[b] + ratio * smooth[b]
-    for copy in first + side_copies + second:
-        copy.wait_send()
+        outs[1, :, c] = out
+        outs[2, :, c] = out * inverse[b] + ratio * smooth[b]
+    for phase in range(3):
+        all_of(phase, send_sem)
     pltpu.make_async_copy(parts, parts, part_send).wait()
 
 
-def deliver(*refs):
-    copies = [pltpu.make_async_copy(refs[n], refs[3 + n], refs[6].at[n]) for n in range(3)]
-    for copy in copies:
-        copy.start()
-    for copy in copies:
-        copy.wait()
+def deliver(stacked, *refs):
+    for n in range(3):
+        pltpu.make_async_copy(stacked.at[n], refs[n], refs[3]).start()
+    pltpu.make_async_copy(stacked, stacked, refs[3]).wait()
 
 
 def on_device(solution, residual, direction, geometry, mass):
@@ -318,11 +336,11 @@
     f32, bf16 = jnp.float32, jnp.bfloat16
     table = jnp.asarray(tables())
     h = rows // 2
-    outs = pl.pallas_call(
+    stacked = pl.pallas_call(
         functools.partial(kernel, ng, nd, ez),
-        out_shape=[pltpu.VMEM(flat, f32)] * 3,
+        out_shape=pltpu.VMEM((3,) + flat, f32),
         in_specs=[pl.BlockSpec(memory_space=pltpu.HBM)] * 6,
-        out_specs=[pl.BlockSpec(memory_space=pltpu.VMEM)] * 3,
+        out_specs=pl.BlockSpec(memory_space=pltpu.VMEM),
         scratch_shapes=[
             pltpu.VMEM(flat, f32),
             pltpu.VMEM(flat, f32),
@@ -330,15 +348,13 @@
             pltpu.VMEM((3,) + flat, bf16),
             pltpu.VMEM(flat, bf16),
             pltpu.VMEM(table.shape, bf16),
-            pltpu.VMEM((3, 2, h, LANES), f32),
-            pltpu.VMEM((3, 2, h, LANES), f32),
-            pltpu.VMEM((3, 2, ez // 2, LANES), f32),
-            pltpu.VMEM((3, 2, 3, ez // 2, LANES), f32),
+            pltpu.VMEM((3, 2 * h + ez, LANES), f32),
+            pltpu.VMEM((3, 2 * h + 3 * ez, LANES), f32),
             pltpu.VMEM((1, 1, LANES), f32),
             pltpu.VMEM((ng * nd - 1, 1, LANES), f32),
             pltpu.SemaphoreType.DMA((6,)),
-            pltpu.SemaphoreType.DMA((3, 8)),
-            pltpu.SemaphoreType.DMA((3, 8)),
+            pltpu.SemaphoreType.DMA((3,)),
+            pltpu.SemaphoreType.DMA((3,)),
             pltpu.SemaphoreType.DMA,
             pltpu.SemaphoreType.DMA,
         ],
@@ -354,11 +370,11 @@
     outs = pl.pallas_call(
         deliver,
         out_shape=[jax.ShapeDtypeStruct(flat, f32)] * 3,
-        in_specs=[pl.BlockSpec(memory_space=pl.ANY)] * 3,
+        in_specs=[pl.BlockSpec(memory_space=pl.ANY)],
         out_specs=[pl.BlockSpec(memory_space=pltpu.HBM)] * 3,
-        scratch_shapes=[pltpu.SemaphoreType.DMA((3,))],
+        scratch_shapes=[pltpu.SemaphoreType.DMA],
         compiler_params=pltpu.CompilerParams(vmem_limit_bytes=8 << 20),
-    )(*outs)
+    )(stacked)
     return tuple(x.reshape(dims) for x in outs)
 
 

time: 21 us -> 20.6 us (0.981)
  Pallas kernels: 20.2 us -> 19.8 us
    pallas_call x1, Pallas kernels: 19.5 us -> 19.1 us  [on_device(): pl.pallas_call(functools.partial(kernel, ng, nd, ez), out_shape=pltpu.VME...]
where the time goes in v1:
time: 20.6 us; the launch traced here: 20.4 us
  Pallas kernels  19.8 us (96%)
  between operations  0.64 us (3%)
    pallas_call x1, Pallas kernels, on_device(): pl.pallas_call(functools.partial(kernel, ng, nd, ez), out_shape=pltpu.VME...  19.1 us
    pallas_call x1, Pallas kernels, on_device(): pl.pallas_call(deliver, out_shape=[jax.ShapeDtypeStruct(flat, f32)] * 3,...  0.68 us

profile of v1, /device:TPU:0, one launch (start us, length us, event | category | flops | bytes accessed | tf_op | source)
XLA Modules:
  0.0 20.4 jit_solution(5780901315541632988)
XLA Ops:
  0.6 19.1 %shard_map.85.stacked = f32[3,32,512]{2,1,0:T(8,128)S(1)} custom-call(f32[32,512]{1,0:T(8,128)} %bitcast.9, f32[32,512]{1,0:T(8,128)} %bitcast.10, f32[32,512]{1,0:T(8,128)} %bitcast.11, bf16[3,32,512]{2,1,0:T(8,128)(2,1)} %bitcast.8, bf16[32,512]{1,0:T(8,128)(2,1)} %bitcast.12, bf16[256,1024]{1,0:T(8,128)(2,1)} %constant.2.clone.tab_h), custom_call_target="tpu_custom_call" | custom-call | tf_op jit(solution)/shard_map/pallas_call | solution.py:339
  19.7 0.7 %shard_map.86 = (f32[32,512]{1,0:T(8,128)}, f32[32,512]{1,0:T(8,128)}, f32[32,512]{1,0:T(8,128)}) custom-call(f32[3,32,512]{2,1,0:T(8,128)S(1)} %shard_map.85.stacked), custom_call_target="tpu_custom_call" | custom-call | tf_op jit(solution)/shard_map/pallas_call | solution.py:370

commit v2 on v1

--- a/solution.py
+++ b/solution.py
@@ -112,32 +112,17 @@
     return out
 
 
-def unpack_j_face(m, b, shift):
-    return jnp.concatenate([roll(m, shift - 8 * b), roll(m, shift - 8 * b - 32)], axis=0)
-
-
-def join_j_faces(mine, before, after):
-    lane = lane_of(mine.shape)
-    first = (lane < 64) & ((lane & 31) < 8)
-    last = (lane >= 64) & ((lane & 31) >= 24)
-    return mine + jnp.where(first, roll(before, 40), jnp.where(last, roll(after, 88), 0.0))
-
-
-def finish_assembly(blocks, ez, i_prev, i_next, j_prev, j_next):
+def assemble_inside(blocks, ez):
     rows = blocks[0].shape[0]
     lane = lane_of((rows, LANES))
-    low = lane < 64
     j, k = (lane >> 3) & 7, lane & 7
-    blocks = list(blocks)
-    blocks[0] = blocks[0] + jnp.where(low, unpack_i_face(i_prev, 0), 0.0)
-    blocks[3] = blocks[3] + jnp.where(low, 0.0, unpack_i_face(i_next, 1))
     outs = []
-    for b, x in enumerate(blocks):
-        after, before = unpack_j_face(j_next, b, 56), unpack_j_face(j_prev, b, 0)
+    for x in blocks:
         if rows > ez:
-            after = jnp.concatenate([roll(x[ez:], 56), after], axis=0)
-            before = jnp.concatenate([before, roll(x[:-ez], -56)], axis=0)
-        x = x + jnp.where(j == 7, after, jnp.where(j == 0, before, 0.0))
+            edge = jnp.zeros((ez, LANES), jnp.float32)
+            after = jnp.concatenate([roll(x[ez:], 56), edge], axis=0)
+            before = jnp.concatenate([edge, roll(x[:-ez], -56)], axis=0)
+            x = x + jnp.where(j == 7, after, jnp.where(j == 0, before, 0.0))
         up, down = roll(x, 7), roll(x, -7)
         after = [pltpu.roll(up[e : e + ez], ez - 1, 0) for e in range(0, rows, ez)]
         before = [pltpu.roll(down[e : e + ez], 1, 0) for e in range(0, rows, ez)]
@@ -146,6 +131,38 @@
     return outs
 
 
+def add_i_face(blocks, message, side):
+    blocks = list(blocks)
+    low = lane_of(blocks[0].shape) < 64
+    face = unpack_i_face(message, side)
+    blocks[3 * side] = blocks[3 * side] + jnp.where(low if side == 0 else ~low, face, 0.0)
+    return blocks
+
+
+def add_j_face(blocks, ez, same, before, after, side):
+    lane = lane_of((ez, LANES))
+    here = ((lane >> 3) & 7) == 7 * side
+
+    def spread(message, shift):
+        return jnp.concatenate([roll(message, shift), roll(message, shift - 32)], axis=0)
+
+    outs = []
+    for b, x in enumerate(blocks):
+        shift = 56 * side - 8 * b
+        face = jnp.where(here, spread(same, shift), 0.0)
+        if b == 0:
+            face = face + jnp.where(here & (lane < 64), spread(before, shift + 40), 0.0)
+        if b == 3:
+            face = face + jnp.where(here & (lane >= 64), spread(after, shift + 88), 0.0)
+        if x.shape[0] == ez:
+            outs.append(x + face)
+        elif side == 0:
+            outs.append(jnp.concatenate([x[:ez] + face, x[ez:]], axis=0))
+        else:
+            outs.append(jnp.concatenate([x[:-ez], x[-ez:] + face], axis=0))
+    return outs
+
+
 def halves(x):
     high = x.astype(jnp.bfloat16)
     return high, (x - high.astype(jnp.float32)).astype(jnp.bfloat16)
@@ -162,6 +179,17 @@
 def total_of(blocks):
     x = blocks[0] + blocks[1] + (blocks[2] + blocks[3])
     return jnp.sum(jnp.sum(x, axis=0, keepdims=True), axis=1, keepdims=True)
+
+
+def owner_weights(rows, ez, first_owned, last_owned):
+    lane = lane_of((rows, LANES))
+    row = lax.broadcasted_iota(jnp.int32, (rows, LANES), 0)
+    k, j = lane & 7, (lane >> 3) & 7
+    base = jnp.where((k == 0) | (k == 7), 0.5, 1.0)
+    first = jnp.where(row < ez, jnp.where(first_owned, 1.0, 0.0), 0.5)
+    last = jnp.where(row >= rows - ez, jnp.where(last_owned, 1.0, 0.0), 0.5)
+    base = base * jnp.where(j == 0, first, jnp.where(j == 7, last, 1.0))
+    return [jnp.where(lane < 64, 0.0, base), base, base, base]
 
 
 def kernel(
@@ -169,8 +197,8 @@
     sol_h, res_h, dir_h, geo_h, mass_h, tab_h,
     outs,
     sol_v, res_v, dir_v, geo_v, mass_v, tab_v,
-    face_out, face_in, part, parts,
-    load_sem, send_sem, recv_sem, part_send, part_recv,
+    face_out, face_in, wrap_in, root_in, prev_v, next_v, part, parts, late_out, late,
+    load_sem, send_sem, recv_sem, last_recv, root_send, root_recv, part_send, part_recv, late_send, go,
 ):
     me_g, me_d = lax.axis_index("group"), lax.axis_index("dev")
 
@@ -184,72 +212,97 @@
     loads = [pltpu.make_async_copy(h, v, load_sem.at[n]) for n, (h, v) in enumerate(pairs)]
     loads[0].start()
     barrier = pltpu.get_barrier_semaphore()
-    for a, b in others:
+    partners = [t for t in others if min(t[0], ng - t[0]) < 2 and min(t[1], nd - t[1]) < 2]
+    hub = (1 % ng, nd // 2)
+    hub_a, hub_b = lax.rem(me_g - hub[0] + ng, ng), lax.rem(me_d - hub[1] + nd, nd)
+    at_hub = (hub_a == 0) & (hub_b == 0)
+    near_hub = ((hub_a < 2) | (hub_a == ng - 1)) & ((hub_b < 2) | (hub_b == nd - 1))
+    for a, b in partners:
         pl.semaphore_signal(barrier, inc=1, device_id=at(a, b), device_id_type=MESH)
+
+    @pl.when(jnp.logical_not(near_hub))
+    def _():
+        pl.semaphore_signal(barrier, inc=1, device_id=hub, device_id_type=MESH)
 
     for load in loads[1:]:
         load.start()
 
     rows = dir_v.shape[0]
     h, q = rows // 2, ez // 2
-
-    def window(ref, phase, start, size):
-        return ref.at[phase, pl.ds(start, size)]
+    is_first, is_last = me_d == 0, me_d == nd - 1
+    owns_next = me_d < nd - 2
 
     def i_out(phase, side):
-        return window(face_out, phase, h * side, h)
+        return face_out.at[phase, pl.ds(h * side, h)]
 
     def i_in(phase, side):
-        return window(face_in, phase, h * side, h)
+        return face_in.at[phase, pl.ds(h * side, h)]
 
     def j_out(phase, side):
-        return window(face_out, phase, 2 * h + q * side, q)
+        return face_out.at[phase, pl.ds(2 * h + q * side, q)]
 
     def j_in(phase, side, turn):
-        return window(face_in, phase, 2 * h + q * (3 * side + turn), q)
-
-    def all_of(phase, sem):
-        pltpu.make_async_copy(face_in.at[phase], face_in.at[phase], sem.at[phase]).wait()
+        return face_in.at[phase, pl.ds(2 * h + q * (3 * side + turn), q)]
+
+    def slot(ref, part_of, group):
+        return ref.at[pl.ds(pl.multiple_of(q * (ng * part_of + group), q), q)]
+
+    def drain(count, sem):
+        source = face_in.at[0] if count <= face_in.shape[1] else root_in
+        ref = source.at[pl.ds(0, count)]
+        pltpu.make_async_copy(ref, ref, sem).wait()
+
+    def drain_phases(start, count, sem):
+        ref = face_in.at[pl.ds(start, count)]
+        pltpu.make_async_copy(ref, ref, sem).wait()
+
+    def send(src, dst, send_to, recv_to, target):
+        return pltpu.make_async_remote_copy(
+            src_ref=src, dst_ref=dst, send_sem=send_to, recv_sem=recv_to,
+            device_id=target, device_id_type=MESH,
+        )
 
     weights = weights_of(rows)
     cut = [slice(LANES * b, LANES * b + LANES) for b in range(4)]
 
-    def exchange(phase, blocks, started=True):
-        made = []
-
-        def give(src, dst, target):
-            made.append(
-                pltpu.make_async_remote_copy(
-                    src_ref=src, dst_ref=dst,
-                    send_sem=send_sem.at[phase], recv_sem=recv_sem.at[phase],
-                    device_id=target, device_id_type=MESH,
-                )
-            )
-            if started:
-                made[-1].start()
-
+    def pack(phase, blocks):
+        for side in range(2):
+            j_out(phase, side)[...] = pack_j_face(blocks, ez, side)
+            i_out(phase, side)[...] = pack_i_face(blocks[3 * side], side)
+
+    def give_j(phase, side, step, sem):
+        for turn, a in ((0, -1), (2, 1), (1, 0)):
+            send(j_out(phase, side), j_in(phase, side, turn), send_sem.at[phase], sem, at(a, step)).start()
+
+    def give_i(phase, sems):
         for side, step in ((0, -1), (1, 1)):
-            i_out(phase, side)[...] = pack_i_face(blocks[3 * side], side)
-            give(i_out(phase, side), i_in(phase, side), at(step, 0))
-        for side, step in ((1, 1), (0, -1)):
-            j_out(phase, side)[...] = pack_j_face(blocks, ez, side)
-            for turn, a in ((0, -1), (2, 1), (1, 0)):
-                give(j_out(phase, side), j_in(phase, side, turn), at(a, step))
-        return made
+            send(i_out(phase, side), i_in(phase, side), send_sem.at[phase], sems[side], at(step, 0)).start()
+
+    def give(phase):
+        give_j(phase, 0, -1, recv_sem.at[phase])
+        give_j(phase, 1, 1, recv_sem.at[phase])
+        give_i(phase, [recv_sem.at[phase]] * 2)
+
+    def turns(phase, side):
+        return [j_in(phase, side, turn)[...] for turn in (1, 2, 0)]
 
     def assembled(phase, blocks):
-        j_prev = join_j_faces(*(j_in(phase, 1, turn)[...] for turn in (1, 2, 0)))
-        j_next = join_j_faces(*(j_in(phase, 0, turn)[...] for turn in (1, 2, 0)))
-        return finish_assembly(blocks, ez, i_in(phase, 1)[...], i_in(phase, 0)[...], j_prev, j_next)
+        blocks = add_i_face(add_i_face(blocks, i_in(phase, 1)[...], 0), i_in(phase, 0)[...], 1)
+        return add_j_face(add_j_face(blocks, ez, *turns(phase, 1), 0), ez, *turns(phase, 0), 1)
 
     d = derivative_table().astype(np.float32)
     loads[0].wait()
-    weighted = [weights[b] * dir_v[:, cut[b]] for b in range(4)]
-    first = exchange(0, weighted, started=False)
-    pl.semaphore_wait(barrier, len(others))
-    for copy in first:
-        copy.start()
-    for load in loads[1:4]:
+    weighted = assemble_inside([weights[b] * dir_v[:, cut[b]] for b in range(4)], ez)
+    pack(0, weighted)
+    pl.semaphore_wait(barrier, jnp.where(at_hub, len(others), len(partners)))
+    give(0)
+
+    @pl.when(at_hub)
+    def _():
+        for a, b in others:
+            pl.semaphore_signal(go, inc=1, device_id=at(a, b), device_id_type=MESH)
+
+    for load in loads[1:5]:
         load.wait()
     geo_rows = stack([jnp.concatenate([geo_v[1, :, c], geo_v[2, :, c]], axis=1) for c in cut])
     squared = dot(geo_rows, tab_v[:, 768:1024])
@@ -258,10 +311,22 @@
     mass = [mass_v[:, c].astype(jnp.float32) for c in cut]
     diag = along_i((d * d).T, geo[0])
     diag = [diag[b] + squared[rows * b : rows * b + rows] + mass[b] for b in range(4)]
-    exchange(1, diag)
-    loads[4].wait()
+    diag = assemble_inside(diag, ez)
+    pack(1, diag)
+    give(1)
+    residual = [res_v[:, c] for c in cut]
+    spread_res = [weights[b] * residual[b] for b in range(4)]
+    mixed = assemble_inside(spread_res, ez)
+    pack(2, mixed)
+    give(2)
     loads[5].wait()
-    all_of(0, recv_sem)
+    owned = owner_weights(rows, ez, is_last, owns_next)
+
+    @pl.when(jnp.logical_not(at_hub))
+    def _():
+        pl.semaphore_wait(go, 1)
+
+    drain_phases(0, 1, recv_sem.at[0])
     smooth = assembled(0, weighted)
 
     high, low = halves(stack(smooth))
@@ -279,18 +344,76 @@
     local = along_i(d.T, flux_i)
     local = [local[b] + back[rows * b : rows * b + rows] + mass[b] * smooth[b] for b in range(4)]
 
-    exchange(2, local)
-    all_of(1, recv_sem)
+    inside = assemble_inside(local, ez)
+    pack(3, inside)
+
+    @pl.when(is_last)
+    def _():
+        for g in range(ng):
+            send(j_out(3, 1), slot(wrap_in, 0, me_g), root_send, root_recv.at[0], (g, 0)).start()
+
+    give_i(3, [last_recv.at[0], last_recv.at[1]])
+    give_j(3, 0, -1, last_recv.at[2])
+
+    @pl.when(jnp.logical_not(is_last))
+    def _():
+        give_j(3, 1, 1, last_recv.at[3])
+
+    @pl.when(is_first)
+    def _():
+        for a in range(1, ng):
+            send(j_out(3, 0), slot(root_in, 0, me_g), root_send, root_recv.at[1], at(a, 0)).start()
+
+    drain_phases(1, 1, recv_sem.at[1])
     inverse = [1.0 / x for x in assembled(1, diag)]
-    residual = [res_v[:, c] for c in cut]
-    scaled = [residual[b] * inverse[b] for b in range(4)]
-    norm_now = total_of([weights[b] * residual[b] * scaled[b] for b in range(4)])
+
+    @pl.when(is_first)
+    def _():
+        lane = lane_of((q, LANES))
+        ends = ((lane & 7) == 0) | ((lane & 7) == 7)
+        share = jnp.where((lane < 64) & ((lane & 31) < 8), 0.0, jnp.where(ends, 0.5, 1.0))
+        face_out[1, pl.ds(2 * h + 2 * q, q)] = share * pack_j_face(inverse, ez, 0)
+        mine = face_out.at[1, pl.ds(2 * h + 2 * q, q)]
+        for a in range(1, ng):
+            send(mine, slot(root_in, 1, me_g), root_send, root_recv.at[1], at(a, 0)).start()
+
+    drain_phases(2, 1, recv_sem.at[2])
+    dual = assembled(2, mixed)
+    norm_now = total_of([spread_res[b] * residual[b] * inverse[b] for b in range(4)])
     curvature = total_of([smooth[b] * local[b] for b in range(4)])
-    all_of(2, recv_sem)
-    applied = assembled(2, local)
-    shared = [weights[b] * applied[b] for b in range(4)]
-    cross = total_of([shared[b] * scaled[b] for b in range(4)])
-    quad = total_of([shared[b] * applied[b] * inverse[b] for b in range(4)])
+    cross = total_of([local[b] * dual[b] * inverse[b] for b in range(4)])
+    share = [owned[b] * inverse[b] for b in range(4)]
+
+    def hold(ref, side):
+        for n, value in enumerate(turns(3, side)):
+            ref[pl.ds(q * n, q)] = value
+
+    def held(ref):
+        return [ref[pl.ds(q * n, q)] for n in range(3)]
+
+    drain(h, last_recv.at[0])
+    closed = add_i_face(inside, i_in(3, 0)[...], 1)
+
+    @pl.when(owns_next)
+    def _():
+        drain(3 * q, last_recv.at[2])
+        hold(next_v, 0)
+
+    @pl.when(jnp.logical_not(owns_next))
+    def _():
+        next_v[...] = jnp.zeros_like(next_v)
+
+    @pl.when(is_last)
+    def _():
+        drain(3 * q, last_recv.at[3])
+        hold(prev_v, 1)
+
+    @pl.when(jnp.logical_not(is_last))
+    def _():
+        prev_v[...] = jnp.zeros_like(prev_v)
+
+    mostly = add_j_face(add_j_face(closed, ez, *held(prev_v), 0), ez, *held(next_v), 1)
+    quad = total_of([share[b] * mostly[b] * mostly[b] for b in range(4)])
 
     lane = lane_of((1, LANES))
     mine = jnp.where(
@@ -300,14 +423,59 @@
     order = sorted(range(len(others)), key=lambda n: (others[n][1] != 0, others[n][1] != 1))
     for n in order:
         a, b = others[n]
-        pltpu.make_async_remote_copy(
-            src_ref=part.at[0], dst_ref=parts.at[n],
-            send_sem=part_send, recv_sem=part_recv,
-            device_id=at(a, b), device_id_type=MESH,
-        ).start()
+        send(part.at[0], parts.at[n], part_send, part_recv, at(a, b)).start()
+
+    @pl.when(is_first)
+    def _():
+        slot(root_in, 0, me_g)[...] = j_out(3, 0)[...]
+        slot(root_in, 1, me_g)[...] = face_out[1, pl.ds(2 * h + 2 * q, q)]
+        drain(2 * (ng - 1) * q, root_recv.at[1])
+        drain(ng * q, root_recv.at[0])
+        spot = lane_of((q, LANES))
+        seam = (spot >= 64) & ((spot & 31) >= 24)
+        faces = [wrap_in[pl.ds(q * g, q)] + root_in[pl.ds(q * g, q)] for g in range(ng)]
+        total = None
+        for g in range(ng):
+            face = faces[g] + jnp.where(seam, roll(faces[(g + 1) % ng], 88), 0.0)
+            term = face * face * root_in[pl.ds(q * (ng + g), q)]
+            total = term if total is None else total + term
+        total = jnp.sum(jnp.sum(total, axis=0, keepdims=True), axis=1, keepdims=True)
+        late[0] = jnp.broadcast_to(total, (1, LANES))
+        late_out[0] = jnp.broadcast_to(total, (1, LANES))
+        for n, shift in enumerate((0, ng - 1, 1)):
+            prev_v[pl.ds(q * n, q)] = slot(wrap_in, 0, lax.rem(me_g + shift, ng))[...]
+
+    speaks = is_first & ((me_g & 1) == 1)
+
+    @pl.when(speaks)
+    def _():
+        for b in range(1, nd):
+            for a in (0, -1):
+                send(late_out.at[0], late.at[0], late_send, root_recv.at[2], at(a, b)).start()
+
+    drain(h, last_recv.at[1])
+
+    @pl.when(jnp.logical_not(owns_next))
+    def _():
+        drain(3 * q, last_recv.at[2])
+        hold(next_v, 0)
+
+    @pl.when(jnp.logical_not(is_last | is_first))
+    def _():
+        drain(3 * q, last_recv.at[3])
+        hold(prev_v, 1)
+
+    applied = add_i_face(closed, i_in(3, 1)[...], 0)
+    applied = add_j_face(add_j_face(applied, ez, *held(prev_v), 0), ez, *held(next_v), 1)
+
+    @pl.when(jnp.logical_not(is_first))
+    def _():
+        pltpu.make_async_copy(late, late, root_recv.at[2]).wait()
+
     pltpu.make_async_copy(parts, parts, part_recv).wait()
     everyone = mine + jnp.sum(parts[...], axis=0)
     norm_now, curvature, cross, quad = (everyone[:, 32 * n : 32 * n + 1] for n in range(4))
+    quad = quad + late[0][:, :1]
     step = norm_now / curvature
     norm_next = norm_now - 2.0 * step * cross + step * step * quad
     ratio = norm_next / norm_now
@@ -317,7 +485,26 @@
         outs[1, :, c] = out
         outs[2, :, c] = out * inverse[b] + ratio * smooth[b]
     for phase in range(3):
-        all_of(phase, send_sem)
+        drain_phases(phase, 1, send_sem.at[phase])
+
+    @pl.when(jnp.logical_not(is_last))
+    def _():
+        drain(2 * h + 6 * q, send_sem.at[3])
+
+    @pl.when(is_last)
+    def _():
+        drain(2 * h + 3 * q, send_sem.at[3])
+        drain(ng * q, root_send)
+
+    @pl.when(is_first)
+    def _():
+        drain(2 * (ng - 1) * q, root_send)
+
+    @pl.when(speaks)
+    def _():
+        ref = parts.at[pl.ds(0, 2 * (nd - 1))]
+        pltpu.make_async_copy(ref, ref, late_send).wait()
+
     pltpu.make_async_copy(parts, parts, part_send).wait()
 
 
@@ -335,7 +522,7 @@
     flat = (rows, points)
     f32, bf16 = jnp.float32, jnp.bfloat16
     table = jnp.asarray(tables())
-    h = rows // 2
+    h, q = rows // 2, ez // 2
     stacked = pl.pallas_call(
         functools.partial(kernel, ng, nd, ez),
         out_shape=pltpu.VMEM((3,) + flat, f32),
@@ -348,15 +535,26 @@
             pltpu.VMEM((3,) + flat, bf16),
             pltpu.VMEM(flat, bf16),
             pltpu.VMEM(table.shape, bf16),
-            pltpu.VMEM((3, 2 * h + ez, LANES), f32),
-            pltpu.VMEM((3, 2 * h + 3 * ez, LANES), f32),
+            pltpu.VMEM((4, 2 * h + 3 * q, LANES), f32),
+            pltpu.VMEM((4, 2 * h + 3 * ez, LANES), f32),
+            pltpu.VMEM((ng * q, LANES), f32),
+            pltpu.VMEM((2 * ng * q, LANES), f32),
+            pltpu.VMEM((3 * q, LANES), f32),
+            pltpu.VMEM((3 * q, LANES), f32),
             pltpu.VMEM((1, 1, LANES), f32),
             pltpu.VMEM((ng * nd - 1, 1, LANES), f32),
+            pltpu.VMEM((1, 1, LANES), f32),
+            pltpu.VMEM((1, 1, LANES), f32),
             pltpu.SemaphoreType.DMA((6,)),
+            pltpu.SemaphoreType.DMA((4,)),
             pltpu.SemaphoreType.DMA((3,)),
+            pltpu.SemaphoreType.DMA((4,)),
+            pltpu.SemaphoreType.DMA,
             pltpu.SemaphoreType.DMA((3,)),
             pltpu.SemaphoreType.DMA,
             pltpu.SemaphoreType.DMA,
+            pltpu.SemaphoreType.DMA,
+            pltpu.SemaphoreType.REGULAR,
         ],
         compiler_params=pltpu.CompilerParams(collective_id=0, has_side_effects=True, vmem_limit_bytes=8 << 20),
     )(

time: 20.6 us -> 19.9 us (0.966)
  Pallas kernels: 19.8 us -> 19.1 us
    pallas_call x1, Pallas kernels: 19.1 us -> 18.4 us  [on_device(): pl.pallas_call(functools.partial(kernel, ng, nd, ez), out_shape=pltpu.VME...]
where the time goes in v2:
time: 19.9 us; the launch traced here: 19.7 us
  Pallas kernels  19.1 us (96%)
  between operations  0.64 us (3%)
    pallas_call x1, Pallas kernels, on_device(): pl.pallas_call(functools.partial(kernel, ng, nd, ez), out_shape=pltpu.VME...  18.4 us
    pallas_call x1, Pallas kernels, on_device(): pl.pallas_call(deliver, out_shape=[jax.ShapeDtypeStruct(flat, f32)] * 3,...  0.68 us

profile of v2, /device:TPU:0, one launch (start us, length us, event | category | flops | bytes accessed | tf_op | source)
XLA Modules:
  0.0 19.7 jit_solution(12756249717351137246)
XLA Ops:
  0.6 18.4 %shard_map.85.stacked = f32[3,32,512]{2,1,0:T(8,128)S(1)} custom-call(f32[32,512]{1,0:T(8,128)} %bitcast.9, f32[32,512]{1,0:T(8,128)} %bitcast.10, f32[32,512]{1,0:T(8,128)} %bitcast.11, bf16[3,32,512]{2,1,0:T(8,128)(2,1)} %bitcast.8, bf16[32,512]{1,0:T(8,128)(2,1)} %bitcast.12, bf16[256,1024]{1,0:T(8,128)(2,1)} %constant.2.clone.tab_h), custom_call_target="tpu_custom_call" | custom-call | tf_op jit(solution)/shard_map/pallas_call | solution.py:526
  19.0 0.7 %shard_map.86 = (f32[32,512]{1,0:T(8,128)}, f32[32,512]{1,0:T(8,128)}, f32[32,512]{1,0:T(8,128)}) custom-call(f32[3,32,512]{2,1,0:T(8,128)S(1)} %shard_map.85.stacked), custom_call_target="tpu_custom_call" | custom-call | tf_op jit(solution)/shard_map/pallas_call | solution.py:568

commit v3 on v2

--- a/solution.py
+++ b/solution.py
@@ -181,7 +181,7 @@
     return jnp.sum(jnp.sum(x, axis=0, keepdims=True), axis=1, keepdims=True)
 
 
-def owner_weights(rows, ez, first_owned, last_owned):
+def owner_weights(rows, ez, first_owned, last_owned, high_owned):
     lane = lane_of((rows, LANES))
     row = lax.broadcasted_iota(jnp.int32, (rows, LANES), 0)
     k, j = lane & 7, (lane >> 3) & 7
@@ -189,16 +189,17 @@
     first = jnp.where(row < ez, jnp.where(first_owned, 1.0, 0.0), 0.5)
     last = jnp.where(row >= rows - ez, jnp.where(last_owned, 1.0, 0.0), 0.5)
     base = base * jnp.where(j == 0, first, jnp.where(j == 7, last, 1.0))
-    return [jnp.where(lane < 64, 0.0, base), base, base, base]
+    high = jnp.where(high_owned, 1.0, 0.0)
+    return [jnp.where(lane < 64, 0.0, base), base, base, jnp.where(lane < 64, base, high * base)]
 
 
 def kernel(
     ng, nd, ez,
     sol_h, res_h, dir_h, geo_h, mass_h, tab_h,
     outs,
-    sol_v, res_v, dir_v, geo_v, mass_v, tab_v,
-    face_out, face_in, wrap_in, root_in, prev_v, next_v, part, parts, late_out, late,
-    load_sem, send_sem, recv_sem, last_recv, root_send, root_recv, part_send, part_recv, late_send, go,
+    pair_v, dir_v, geo_v, tab_v,
+    face_out, face_in, wrap_in, root_in, side_in, side_out, prev_v, next_v, high_v, part, parts, late_out, late,
+    load_sem, send_sem, recv_sem, side_recv, last_recv, root_recv, part_recv, go,
 ):
     me_g, me_d = lax.axis_index("group"), lax.axis_index("dev")
 
@@ -208,8 +209,11 @@
     others = [(a, b) for a in range(ng) for b in range(nd) if (a, b) != (0, 0)]
     others.sort(key=lambda t: (min(t[1], nd - t[1]) != 1, min(t[0], ng - t[0]) > 1))
 
-    pairs = ((dir_h, dir_v), (geo_h, geo_v), (mass_h, mass_v), (tab_h, tab_v), (res_h, res_v), (sol_h, sol_v))
-    loads = [pltpu.make_async_copy(h, v, load_sem.at[n]) for n, (h, v) in enumerate(pairs)]
+    pairs = (
+        (dir_h, dir_v, 0), (geo_h, geo_v.at[pl.ds(0, 3)], 1), (mass_h, geo_v.at[3], 1),
+        (tab_h, tab_v, 2), (res_h, pair_v.at[0], 3), (sol_h, pair_v.at[1], 3),
+    )
+    loads = [pltpu.make_async_copy(h, v, load_sem.at[n]) for h, v, n in pairs]
     loads[0].start()
     barrier = pltpu.get_barrier_semaphore()
     partners = [t for t in others if min(t[0], ng - t[0]) < 2 and min(t[1], nd - t[1]) < 2]
@@ -229,36 +233,34 @@
 
     rows = dir_v.shape[0]
     h, q = rows // 2, ez // 2
-    is_first, is_last = me_d == 0, me_d == nd - 1
+    u, span = h + q, 2 * h + 6 * q
+    is_first, is_last, is_near = me_d == 0, me_d == nd - 1, me_d == nd - 2
+    odd = (me_g & 1) == 1
     owns_next = me_d < nd - 2
+    owns_high = jnp.logical_not(is_last & odd)
 
     def i_out(phase, side):
-        return face_out.at[phase, pl.ds(h * side, h)]
+        return face_out.at[phase, pl.ds(u * side, h)]
 
     def i_in(phase, side):
-        return face_in.at[phase, pl.ds(h * side, h)]
+        return face_in.at[pl.ds(span * phase + h * side, h)]
 
     def j_out(phase, side):
-        return face_out.at[phase, pl.ds(2 * h + q * side, q)]
+        return face_out.at[phase, pl.ds(2 * h + q if side == 0 else h, q)]
 
     def j_in(phase, side, turn):
-        return face_in.at[phase, pl.ds(2 * h + q * (3 * side + turn), q)]
+        return face_in.at[pl.ds(span * phase + 2 * h + q * (3 * side + turn), q)]
 
     def slot(ref, part_of, group):
         return ref.at[pl.ds(pl.multiple_of(q * (ng * part_of + group), q), q)]
 
     def drain(count, sem):
-        source = face_in.at[0] if count <= face_in.shape[1] else root_in
-        ref = source.at[pl.ds(0, count)]
+        ref = face_in.at[pl.ds(0, count)]
         pltpu.make_async_copy(ref, ref, sem).wait()
 
-    def drain_phases(start, count, sem):
-        ref = face_in.at[pl.ds(start, count)]
-        pltpu.make_async_copy(ref, ref, sem).wait()
-
-    def send(src, dst, send_to, recv_to, target):
+    def send(src, dst, recv_to, target):
         return pltpu.make_async_remote_copy(
-            src_ref=src, dst_ref=dst, send_sem=send_to, recv_sem=recv_to,
+            src_ref=src, dst_ref=dst, send_sem=send_sem, recv_sem=recv_to,
             device_id=target, device_id_type=MESH,
         )
 
@@ -272,16 +274,16 @@
 
     def give_j(phase, side, step, sem):
         for turn, a in ((0, -1), (2, 1), (1, 0)):
-            send(j_out(phase, side), j_in(phase, side, turn), send_sem.at[phase], sem, at(a, step)).start()
+            send(j_out(phase, side), j_in(phase, side, turn), sem, at(a, step)).start()
 
     def give_i(phase, sems):
         for side, step in ((0, -1), (1, 1)):
-            send(i_out(phase, side), i_in(phase, side), send_sem.at[phase], sems[side], at(step, 0)).start()
-
-    def give(phase):
-        give_j(phase, 0, -1, recv_sem.at[phase])
-        give_j(phase, 1, 1, recv_sem.at[phase])
-        give_i(phase, [recv_sem.at[phase]] * 2)
+            send(i_out(phase, side), i_in(phase, side), sems[side], at(step, 0)).start()
+
+    def give(phase, sems):
+        give_j(phase, 0, -1, sems[2])
+        give_j(phase, 1, 1, sems[3])
+        give_i(phase, sems[:2])
 
     def turns(phase, side):
         return [j_in(phase, side, turn)[...] for turn in (1, 2, 0)]
@@ -295,38 +297,57 @@
     weighted = assemble_inside([weights[b] * dir_v[:, cut[b]] for b in range(4)], ez)
     pack(0, weighted)
     pl.semaphore_wait(barrier, jnp.where(at_hub, len(others), len(partners)))
-    give(0)
+    give(0, [recv_sem.at[0]] * 4)
 
     @pl.when(at_hub)
     def _():
         for a, b in others:
             pl.semaphore_signal(go, inc=1, device_id=at(a, b), device_id_type=MESH)
 
-    for load in loads[1:5]:
-        load.wait()
+    pltpu.make_async_copy(geo_v, geo_v, load_sem.at[1]).wait()
+    loads[3].wait()
     geo_rows = stack([jnp.concatenate([geo_v[1, :, c], geo_v[2, :, c]], axis=1) for c in cut])
     squared = dot(geo_rows, tab_v[:, 768:1024])
     squared = squared[:, :LANES] + squared[:, LANES:]
     geo = [[geo_v[c, :, cut[b]].astype(jnp.float32) for b in range(4)] for c in range(3)]
-    mass = [mass_v[:, c].astype(jnp.float32) for c in cut]
+    mass = [geo_v[3, :, c].astype(jnp.float32) for c in cut]
     diag = along_i((d * d).T, geo[0])
     diag = [diag[b] + squared[rows * b : rows * b + rows] + mass[b] for b in range(4)]
     diag = assemble_inside(diag, ez)
     pack(1, diag)
-    give(1)
-    residual = [res_v[:, c] for c in cut]
+    give(1, [side_recv.at[0], side_recv.at[0], side_recv.at[1], side_recv.at[0]])
+    pltpu.make_async_copy(pair_v, pair_v, load_sem.at[3]).wait()
+    residual = [pair_v[0, :, c] for c in cut]
     spread_res = [weights[b] * residual[b] for b in range(4)]
     mixed = assemble_inside(spread_res, ez)
     pack(2, mixed)
-    give(2)
-    loads[5].wait()
-    owned = owner_weights(rows, ez, is_last, owns_next)
+    give(2, [recv_sem.at[1]] * 4)
+    owned = owner_weights(rows, ez, is_last, owns_next, owns_high)
 
     @pl.when(jnp.logical_not(at_hub))
     def _():
         pl.semaphore_wait(go, 1)
 
-    drain_phases(0, 1, recv_sem.at[0])
+    @pl.when(is_last)
+    def _():
+        drain(2 * h + 3 * q, side_recv.at[0])
+
+    @pl.when(is_last & odd)
+    def _():
+        side = add_i_face(add_i_face(diag, i_in(1, 1)[...], 0), i_in(1, 0)[...], 1)
+        side = [1.0 / x for x in add_j_face(side, ez, *turns(1, 1), 0)]
+        lane = lane_of((h, LANES))
+        row = lax.broadcasted_iota(jnp.int32, (h, LANES), 0) + jnp.where(lane < 64, 0, h)
+        j, k = (lane >> 3) & 7, lane & 7
+        fit = jnp.where(j == 0, jnp.where(row < ez, 1.0, 0.5), 1.0)
+        fit = jnp.where(j == 7, jnp.where(row < rows - ez, 0.5, 0.0), fit)
+        fit = fit * jnp.where((k == 0) | (k == 7), 0.5, 1.0)
+        side_out[...] = fit * pack_i_face(side[3], 1)
+        for g in range(ng):
+            dst = side_in.at[pl.ds(pl.multiple_of((me_g >> 1) * h, q), h)]
+            send(side_out, dst, root_recv.at[1], (g, 0)).start()
+
+    drain(span, recv_sem.at[0])
     smooth = assembled(0, weighted)
 
     high, low = halves(stack(smooth))
@@ -350,7 +371,14 @@
     @pl.when(is_last)
     def _():
         for g in range(ng):
-            send(j_out(3, 1), slot(wrap_in, 0, me_g), root_send, root_recv.at[0], (g, 0)).start()
+            start = pl.multiple_of((me_g & 1) * h, q)
+            dst = wrap_in.at[pl.ds(pl.multiple_of(me_g * u, q), u)]
+            send(face_out.at[3, pl.ds(start, u)], dst, root_recv.at[0], (g, 0)).start()
+
+    @pl.when(is_near)
+    def _():
+        for g in range(ng):
+            send(j_out(3, 1), slot(root_in, 2, me_g), root_recv.at[1], (g, 0)).start()
 
     give_i(3, [last_recv.at[0], last_recv.at[1]])
     give_j(3, 0, -1, last_recv.at[2])
@@ -362,9 +390,13 @@
     @pl.when(is_first)
     def _():
         for a in range(1, ng):
-            send(j_out(3, 0), slot(root_in, 0, me_g), root_send, root_recv.at[1], at(a, 0)).start()
-
-    drain_phases(1, 1, recv_sem.at[1])
+            send(j_out(3, 0), slot(root_in, 0, me_g), root_recv.at[1], at(a, 0)).start()
+
+    @pl.when(jnp.logical_not(is_last))
+    def _():
+        drain(2 * h + 3 * q, side_recv.at[0])
+
+    drain(3 * q, side_recv.at[1])
     inverse = [1.0 / x for x in assembled(1, diag)]
 
     @pl.when(is_first)
@@ -372,12 +404,11 @@
         lane = lane_of((q, LANES))
         ends = ((lane & 7) == 0) | ((lane & 7) == 7)
         share = jnp.where((lane < 64) & ((lane & 31) < 8), 0.0, jnp.where(ends, 0.5, 1.0))
-        face_out[1, pl.ds(2 * h + 2 * q, q)] = share * pack_j_face(inverse, ez, 0)
-        mine = face_out.at[1, pl.ds(2 * h + 2 * q, q)]
+        side_out[pl.ds(0, q)] = share * pack_j_face(inverse, ez, 0)
         for a in range(1, ng):
-            send(mine, slot(root_in, 1, me_g), root_send, root_recv.at[1], at(a, 0)).start()
-
-    drain_phases(2, 1, recv_sem.at[2])
+            send(side_out.at[pl.ds(0, q)], slot(root_in, 1, me_g), root_recv.at[1], at(a, 0)).start()
+
+    drain(span, recv_sem.at[1])
     dual = assembled(2, mixed)
     norm_now = total_of([spread_res[b] * residual[b] * inverse[b] for b in range(4)])
     curvature = total_of([smooth[b] * local[b] for b in range(4)])
@@ -391,8 +422,14 @@
     def held(ref):
         return [ref[pl.ds(q * n, q)] for n in range(3)]
 
-    drain(h, last_recv.at[0])
-    closed = add_i_face(inside, i_in(3, 0)[...], 1)
+    @pl.when(owns_high)
+    def _():
+        drain(h, last_recv.at[0])
+        high_v[...] = i_in(3, 0)[...]
+
+    @pl.when(jnp.logical_not(owns_high))
+    def _():
+        high_v[...] = jnp.zeros_like(high_v)
 
     @pl.when(owns_next)
     def _():
@@ -412,7 +449,8 @@
     def _():
         prev_v[...] = jnp.zeros_like(prev_v)
 
-    mostly = add_j_face(add_j_face(closed, ez, *held(prev_v), 0), ez, *held(next_v), 1)
+    mostly = add_i_face(inside, high_v[...], 1)
+    mostly = add_j_face(add_j_face(mostly, ez, *held(prev_v), 0), ez, *held(next_v), 1)
     quad = total_of([share[b] * mostly[b] * mostly[b] for b in range(4)])
 
     lane = lane_of((1, LANES))
@@ -423,37 +461,64 @@
     order = sorted(range(len(others)), key=lambda n: (others[n][1] != 0, others[n][1] != 1))
     for n in order:
         a, b = others[n]
-        send(part.at[0], parts.at[n], part_send, part_recv, at(a, b)).start()
+        send(part.at[0], parts.at[n], part_recv, at(a, b)).start()
 
     @pl.when(is_first)
     def _():
         slot(root_in, 0, me_g)[...] = j_out(3, 0)[...]
-        slot(root_in, 1, me_g)[...] = face_out[1, pl.ds(2 * h + 2 * q, q)]
-        drain(2 * (ng - 1) * q, root_recv.at[1])
-        drain(ng * q, root_recv.at[0])
+        slot(root_in, 1, me_g)[...] = side_out[pl.ds(0, q)]
+        drain((3 * ng - 2) * q + ng // 2 * h, root_recv.at[1])
+        drain(ng * u, root_recv.at[0])
+
+        def far(g):
+            return wrap_in[pl.ds(u * g + (0 if g & 1 else h), q)]
+
+        def across(g):
+            return wrap_in[pl.ds(u * g + (q if g & 1 else 0), h)]
+
+        def near(g):
+            return root_in[pl.ds(q * (2 * ng + g), q)]
+
         spot = lane_of((q, LANES))
         seam = (spot >= 64) & ((spot & 31) >= 24)
-        faces = [wrap_in[pl.ds(q * g, q)] + root_in[pl.ds(q * g, q)] for g in range(ng)]
+        faces = [far(g) + root_in[pl.ds(q * g, q)] for g in range(ng)]
         total = None
         for g in range(ng):
             face = faces[g] + jnp.where(seam, roll(faces[(g + 1) % ng], 88), 0.0)
             term = face * face * root_in[pl.ds(q * (ng + g), q)]
             total = term if total is None else total + term
+        spot = lane_of((ez, LANES))
+        for g in range(1, ng, 2):
+            one, two = near(g), near((g + 1) % ng)
+            line = jnp.concatenate([roll(one, -88) + two, roll(one, -120) + roll(two, -32)], axis=0)
+            line = jnp.where(spot < 8, line, 0.0)
+            if h > ez:
+                line = jnp.concatenate([line, jnp.zeros((h - ez, LANES), jnp.float32)], axis=0)
+            face = across(g) + across((g + 1) % ng) + line
+            term = face * face * side_in[pl.ds(h * (g // 2), h)]
+            for n in range(0, h, q):
+                total = total + term[n : n + q]
         total = jnp.sum(jnp.sum(total, axis=0, keepdims=True), axis=1, keepdims=True)
         late[0] = jnp.broadcast_to(total, (1, LANES))
         late_out[0] = jnp.broadcast_to(total, (1, LANES))
         for n, shift in enumerate((0, ng - 1, 1)):
-            prev_v[pl.ds(q * n, q)] = slot(wrap_in, 0, lax.rem(me_g + shift, ng))[...]
-
-    speaks = is_first & ((me_g & 1) == 1)
+            g = lax.rem(me_g + shift, ng)
+            prev_v[pl.ds(q * n, q)] = wrap_in[pl.ds(pl.multiple_of(u * g + h * (1 - (g & 1)), q), q)]
+
+    speaks = is_first & odd
 
     @pl.when(speaks)
     def _():
         for b in range(1, nd):
             for a in (0, -1):
-                send(late_out.at[0], late.at[0], late_send, root_recv.at[2], at(a, b)).start()
+                send(late_out.at[0], late.at[0], root_recv.at[2], at(a, b)).start()
 
     drain(h, last_recv.at[1])
+
+    @pl.when(jnp.logical_not(owns_high))
+    def _():
+        drain(h, last_recv.at[0])
+        high_v[...] = i_in(3, 0)[...]
 
     @pl.when(jnp.logical_not(owns_next))
     def _():
@@ -465,7 +530,7 @@
         drain(3 * q, last_recv.at[3])
         hold(prev_v, 1)
 
-    applied = add_i_face(closed, i_in(3, 1)[...], 0)
+    applied = add_i_face(add_i_face(inside, high_v[...], 1), i_in(3, 1)[...], 0)
     applied = add_j_face(add_j_face(applied, ez, *held(prev_v), 0), ez, *held(next_v), 1)
 
     @pl.when(jnp.logical_not(is_first))
@@ -480,32 +545,24 @@
     norm_next = norm_now - 2.0 * step * cross + step * step * quad
     ratio = norm_next / norm_now
     for b, c in enumerate(cut):
-        outs[0, :, c] = sol_v[:, c] + step * smooth[b]
+        outs[0, :, c] = pair_v[1, :, c] + step * smooth[b]
         out = residual[b] - step * applied[b]
         outs[1, :, c] = out
         outs[2, :, c] = out * inverse[b] + ratio * smooth[b]
-    for phase in range(3):
-        drain_phases(phase, 1, send_sem.at[phase])
-
-    @pl.when(jnp.logical_not(is_last))
-    def _():
-        drain(2 * h + 6 * q, send_sem.at[3])
-
-    @pl.when(is_last)
-    def _():
-        drain(2 * h + 3 * q, send_sem.at[3])
-        drain(ng * q, root_send)
-
-    @pl.when(is_first)
-    def _():
-        drain(2 * (ng - 1) * q, root_send)
-
-    @pl.when(speaks)
-    def _():
-        ref = parts.at[pl.ds(0, 2 * (nd - 1))]
-        pltpu.make_async_copy(ref, ref, late_send).wait()
-
-    pltpu.make_async_copy(parts, parts, part_send).wait()
+    common = 4 * span + len(others)
+    roles = [
+        (is_first & odd, 2 * (ng - 1) * q + 2 * (nd - 1)),
+        (is_first & jnp.logical_not(odd), 2 * (ng - 1) * q),
+        (is_last & odd, ng * (u + h) - 3 * q),
+        (is_last & jnp.logical_not(odd), ng * u - 3 * q),
+        (is_near, ng * q),
+        (jnp.logical_not(is_first | is_last | is_near), 0),
+    ]
+    for role, extra in roles:
+
+        @pl.when(role)
+        def _():
+            drain(common + extra, send_sem)
 
 
 def deliver(stacked, *refs):
@@ -523,36 +580,38 @@
     f32, bf16 = jnp.float32, jnp.bfloat16
     table = jnp.asarray(tables())
     h, q = rows // 2, ez // 2
+    u, q8 = h + q, 8
+    spare = 4 * (2 * h + 6 * q) + ng * nd + 2 * nd + ng * (u + h)
+    spare = -(-spare // q8) * q8
     stacked = pl.pallas_call(
         functools.partial(kernel, ng, nd, ez),
         out_shape=pltpu.VMEM((3,) + flat, f32),
         in_specs=[pl.BlockSpec(memory_space=pltpu.HBM)] * 6,
         out_specs=pl.BlockSpec(memory_space=pltpu.VMEM),
         scratch_shapes=[
+            pltpu.VMEM((2,) + flat, f32),
             pltpu.VMEM(flat, f32),
-            pltpu.VMEM(flat, f32),
-            pltpu.VMEM(flat, f32),
-            pltpu.VMEM((3,) + flat, bf16),
-            pltpu.VMEM(flat, bf16),
+            pltpu.VMEM((4,) + flat, bf16),
             pltpu.VMEM(table.shape, bf16),
-            pltpu.VMEM((4, 2 * h + 3 * q, LANES), f32),
-            pltpu.VMEM((4, 2 * h + 3 * ez, LANES), f32),
-            pltpu.VMEM((ng * q, LANES), f32),
-            pltpu.VMEM((2 * ng * q, LANES), f32),
+            pltpu.VMEM((4, 2 * u, LANES), f32),
+            pltpu.VMEM((spare, LANES), f32),
+            pltpu.VMEM((ng * u, LANES), f32),
+            pltpu.VMEM((3 * ng * q, LANES), f32),
+            pltpu.VMEM((ng // 2 * h, LANES), f32),
+            pltpu.VMEM((h, LANES), f32),
             pltpu.VMEM((3 * q, LANES), f32),
             pltpu.VMEM((3 * q, LANES), f32),
+            pltpu.VMEM((h, LANES), f32),
             pltpu.VMEM((1, 1, LANES), f32),
             pltpu.VMEM((ng * nd - 1, 1, LANES), f32),
             pltpu.VMEM((1, 1, LANES), f32),
             pltpu.VMEM((1, 1, LANES), f32),
-            pltpu.SemaphoreType.DMA((6,)),
+            pltpu.SemaphoreType.DMA((4,)),
+            pltpu.SemaphoreType.DMA,
+            pltpu.SemaphoreType.DMA((2,)),
+            pltpu.SemaphoreType.DMA((2,)),
             pltpu.SemaphoreType.DMA((4,)),
             pltpu.SemaphoreType.DMA((3,)),
-            pltpu.SemaphoreType.DMA((4,)),
-            pltpu.SemaphoreType.DMA,
-            pltpu.SemaphoreType.DMA((3,)),
-            pltpu.SemaphoreType.DMA,
-            pltpu.SemaphoreType.DMA,
             pltpu.SemaphoreType.DMA,
             pltpu.SemaphoreType.REGULAR,
         ],

time: 19.9 us -> 18.7 us (0.940)
  Pallas kernels: 19.1 us -> 17.9 us
    pallas_call x1, Pallas kernels: 18.4 us -> 17.3 us  [on_device(): pl.pallas_call(functools.partial(kernel, ng, nd, ez), out_shape=pltpu.VME...]
where the time goes in v3:
time: 18.7 us; the launch traced here: 18.6 us
  Pallas kernels  17.9 us (96%)
  between operations  0.64 us (3%)
    pallas_call x1, Pallas kernels, on_device(): pl.pallas_call(functools.partial(kernel, ng, nd, ez), out_shape=pltpu.VME...  17.3 us
    pallas_call x1, Pallas kernels, on_device(): pl.pallas_call(deliver, out_shape=[jax.ShapeDtypeStruct(flat, f32)] * 3,...  0.68 us

profile of v3, /device:TPU:0, one launch (start us, length us, event | category | flops | bytes accessed | tf_op | source)
XLA Modules:
  0.0 18.6 jit_solution(6650470228025507203)
XLA Ops:
  0.6 17.3 %shard_map.85.stacked = f32[3,32,512]{2,1,0:T(8,128)S(1)} custom-call(f32[32,512]{1,0:T(8,128)} %bitcast.9, f32[32,512]{1,0:T(8,128)} %bitcast.10, f32[32,512]{1,0:T(8,128)} %bitcast.11, bf16[3,32,512]{2,1,0:T(8,128)(2,1)} %bitcast.8, bf16[32,512]{1,0:T(8,128)(2,1)} %bitcast.12, bf16[256,1024]{1,0:T(8,128)(2,1)} %constant.2.clone.tab_h), custom_call_target="tpu_custom_call" | custom-call | tf_op jit(solution)/shard_map/pallas_call | solution.py:586
  17.9 0.7 %shard_map.86 = (f32[32,512]{1,0:T(8,128)}, f32[32,512]{1,0:T(8,128)}, f32[32,512]{1,0:T(8,128)}) custom-call(f32[3,32,512]{2,1,0:T(8,128)S(1)} %shard_map.85.stacked), custom_call_target="tpu_custom_call" | custom-call | tf_op jit(solution)/shard_map/pallas_call | solution.py:627

commit v4 on v3

--- a/solution.py
+++ b/solution.py
@@ -131,6 +131,58 @@
     return outs
 
 
+def turn_column(x, ez, shift):
+    parts = [pltpu.roll(x[e : e + ez], shift % ez, 0) for e in range(0, x.shape[0], ez)]
+    return parts[0] if len(parts) == 1 else jnp.concatenate(parts, axis=0)
+
+
+def summed_j_face(blocks, ez, side):
+    half = ez // 2
+    lane = lane_of((half, LANES))
+    slot, k = (lane & 63) >> 3, lane & 7
+    kept = [jnp.zeros((half, LANES), jnp.float32)] * 3
+    for b in range(4):
+        column = blocks[b][:ez] if side == 0 else blocks[b][-ez:]
+        kinds = ((column, 0), (turn_column(column, ez, -1), 7), (turn_column(column, ez, 1), -7))
+        for n in range(2):
+            shift = 8 * b + 32 * n - 56 * side
+            for m, (rows, extra) in enumerate(kinds):
+                moved = roll(rows[n * half : (n + 1) * half], shift + extra)
+                kept[m] = jnp.where(slot == b + 4 * n, moved, kept[m])
+    return kept[0] + jnp.where(k == 7, kept[1], jnp.where(k == 0, kept[2], 0.0))
+
+
+def summed_i_face(x, ez, side):
+    rows = x.shape[0]
+    h = rows // 2
+    lane = lane_of((h, LANES))
+    j, k = (lane >> 3) & 7, lane & 7
+    edge = jnp.zeros((ez, LANES), jnp.float32)
+
+    def gather(bottom):
+        cut = slice(h, rows) if bottom else slice(0, h)
+        base = 64 if bottom != (side == 1) else 0
+        total = None
+        for column, shift, where in ((0, 0, None), (1, 56, j == 7), (-1, -56, j == 0)):
+            if column and (rows == ez or (rows == 2 * ez and bottom == (column == 1))):
+                continue
+            found = None
+            for turn, extra, only in ((0, 0, None), (-1, 7, k == 7), (1, -7, k == 0)):
+                y = turn_column(x, ez, turn) if turn else x
+                if column == 1:
+                    y = jnp.concatenate([y[ez:], edge], axis=0)
+                elif column == -1:
+                    y = jnp.concatenate([edge, y[:-ez]], axis=0)
+                y = roll(y[cut], base + shift + extra)
+                y = y if only is None else jnp.where(only, y, 0.0)
+                found = y if found is None else found + y
+            found = found if where is None else jnp.where(where, found, 0.0)
+            total = found if total is None else total + found
+        return total
+
+    return jnp.where(lane < 64, gather(False), gather(True))
+
+
 def add_i_face(blocks, message, side):
     blocks = list(blocks)
     low = lane_of(blocks[0].shape) < 64
@@ -190,16 +242,17 @@
     last = jnp.where(row >= rows - ez, jnp.where(last_owned, 1.0, 0.0), 0.5)
     base = base * jnp.where(j == 0, first, jnp.where(j == 7, last, 1.0))
     high = jnp.where(high_owned, 1.0, 0.0)
-    return [jnp.where(lane < 64, 0.0, base), base, base, jnp.where(lane < 64, base, high * base)]
+    outer = [jnp.where(lane < 64, 0.0, base), base, base, jnp.where(lane < 64, base, high * base)]
+    return outer, base
 
 
 def kernel(
     ng, nd, ez,
     sol_h, res_h, dir_h, geo_h, mass_h, tab_h,
     outs,
-    pair_v, dir_v, geo_v, tab_v,
-    face_out, face_in, wrap_in, root_in, side_in, side_out, prev_v, next_v, high_v, part, parts, late_out, late,
-    load_sem, send_sem, recv_sem, side_recv, last_recv, root_recv, part_recv, go,
+    pair_v, dir_v, geo_v, tab_v, early_v,
+    face_out, face_in, wrap_in, root_in, side_in, side_out, prev_v, next_v, low_v, high_v, part, sums, parts, late_out,
+    bulk, load_sem, send_sem, recv_sem, side_recv, last_recv, root_recv, sum_recv, part_recv, go,
 ):
     me_g, me_d = lax.axis_index("group"), lax.axis_index("dev")
 
@@ -211,7 +264,7 @@
 
     pairs = (
         (dir_h, dir_v, 0), (geo_h, geo_v.at[pl.ds(0, 3)], 1), (mass_h, geo_v.at[3], 1),
-        (tab_h, tab_v, 2), (res_h, pair_v.at[0], 3), (sol_h, pair_v.at[1], 3),
+        (tab_h, tab_v, 1), (res_h, pair_v.at[0], 1), (sol_h, pair_v.at[1], 1),
     )
     loads = [pltpu.make_async_copy(h, v, load_sem.at[n]) for h, v, n in pairs]
     loads[0].start()
@@ -235,9 +288,11 @@
     h, q = rows // 2, ez // 2
     u, span = h + q, 2 * h + 6 * q
     is_first, is_last, is_near = me_d == 0, me_d == nd - 1, me_d == nd - 2
+    root = min(1, ng - 1)
+    is_root = is_first & (me_g == root)
     odd = (me_g & 1) == 1
     owns_next = me_d < nd - 2
-    owns_high = jnp.logical_not(is_last & odd)
+    owns_high, owns_low = jnp.logical_not(is_last), is_last & odd
 
     def i_out(phase, side):
         return face_out.at[phase, pl.ds(u * side, h)]
@@ -273,7 +328,7 @@
             i_out(phase, side)[...] = pack_i_face(blocks[3 * side], side)
 
     def give_j(phase, side, step, sem):
-        for turn, a in ((0, -1), (2, 1), (1, 0)):
+        for turn, a in ((2, 1), (0, -1), (1, 0)):
             send(j_out(phase, side), j_in(phase, side, turn), sem, at(a, step)).start()
 
     def give_i(phase, sems):
@@ -297,15 +352,14 @@
     weighted = assemble_inside([weights[b] * dir_v[:, cut[b]] for b in range(4)], ez)
     pack(0, weighted)
     pl.semaphore_wait(barrier, jnp.where(at_hub, len(others), len(partners)))
-    give(0, [recv_sem.at[0]] * 4)
+    give(0, [recv_sem] * 4)
 
     @pl.when(at_hub)
     def _():
         for a, b in others:
             pl.semaphore_signal(go, inc=1, device_id=at(a, b), device_id_type=MESH)
 
-    pltpu.make_async_copy(geo_v, geo_v, load_sem.at[1]).wait()
-    loads[3].wait()
+    pltpu.make_async_copy(bulk, bulk, load_sem.at[1]).wait()
     geo_rows = stack([jnp.concatenate([geo_v[1, :, c], geo_v[2, :, c]], axis=1) for c in cut])
     squared = dot(geo_rows, tab_v[:, 768:1024])
     squared = squared[:, :LANES] + squared[:, LANES:]
@@ -316,38 +370,50 @@
     diag = assemble_inside(diag, ez)
     pack(1, diag)
     give(1, [side_recv.at[0], side_recv.at[0], side_recv.at[1], side_recv.at[0]])
-    pltpu.make_async_copy(pair_v, pair_v, load_sem.at[3]).wait()
     residual = [pair_v[0, :, c] for c in cut]
     spread_res = [weights[b] * residual[b] for b in range(4)]
     mixed = assemble_inside(spread_res, ez)
     pack(2, mixed)
-    give(2, [recv_sem.at[1]] * 4)
-    owned = owner_weights(rows, ez, is_last, owns_next, owns_high)
+    give(2, [side_recv.at[0], side_recv.at[0], side_recv.at[1], side_recv.at[0]])
+    owned, face_owned = owner_weights(rows, ez, is_last, owns_next, owns_high)
 
     @pl.when(jnp.logical_not(at_hub))
     def _():
         pl.semaphore_wait(go, 1)
 
+    def nearly(phase, blocks):
+        blocks = add_i_face(add_i_face(blocks, i_in(phase, 1)[...], 0), i_in(phase, 0)[...], 1)
+        return add_j_face(blocks, ez, *turns(phase, 1), 0)
+
+    def gather_sides():
+        drain(2 * (2 * h + 3 * q), side_recv.at[0])
+        for b, x in enumerate(nearly(1, [early_v[0, :, c] for c in cut])):
+            early_v[0, :, cut[b]] = x
+            early_v[2, :, cut[b]] = 1.0 / x
+        for b, x in enumerate(nearly(2, [early_v[1, :, c] for c in cut])):
+            early_v[1, :, cut[b]] = x
+
+    for b, c in enumerate(cut):
+        early_v[0, :, c] = diag[b]
+        early_v[1, :, c] = mixed[b]
+
     @pl.when(is_last)
     def _():
-        drain(2 * h + 3 * q, side_recv.at[0])
+        gather_sides()
 
     @pl.when(is_last & odd)
     def _():
-        side = add_i_face(add_i_face(diag, i_in(1, 1)[...], 0), i_in(1, 0)[...], 1)
-        side = [1.0 / x for x in add_j_face(side, ez, *turns(1, 1), 0)]
         lane = lane_of((h, LANES))
         row = lax.broadcasted_iota(jnp.int32, (h, LANES), 0) + jnp.where(lane < 64, 0, h)
         j, k = (lane >> 3) & 7, lane & 7
         fit = jnp.where(j == 0, jnp.where(row < ez, 1.0, 0.5), 1.0)
         fit = jnp.where(j == 7, jnp.where(row < rows - ez, 0.5, 0.0), fit)
         fit = fit * jnp.where((k == 0) | (k == 7), 0.5, 1.0)
-        side_out[...] = fit * pack_i_face(side[3], 1)
-        for g in range(ng):
-            dst = side_in.at[pl.ds(pl.multiple_of((me_g >> 1) * h, q), h)]
-            send(side_out, dst, root_recv.at[1], (g, 0)).start()
-
-    drain(span, recv_sem.at[0])
+        side_out[...] = fit * pack_i_face(early_v[2, :, cut[3]], 1)
+        dst = side_in.at[pl.ds(pl.multiple_of((me_g >> 1) * h, q), h)]
+        send(side_out, dst, root_recv, (root, 0)).start()
+
+    drain(span, recv_sem)
     smooth = assembled(0, weighted)
 
     high, low = halves(stack(smooth))
@@ -365,20 +431,33 @@
     local = along_i(d.T, flux_i)
     local = [local[b] + back[rows * b : rows * b + rows] + mass[b] * smooth[b] for b in range(4)]
 
-    inside = assemble_inside(local, ez)
-    pack(3, inside)
+    for side in range(2):
+        j_out(3, side)[...] = summed_j_face(local, ez, side)
+        i_out(3, side)[...] = summed_i_face(local[3 * side], ez, side)
 
     @pl.when(is_last)
     def _():
-        for g in range(ng):
-            start = pl.multiple_of((me_g & 1) * h, q)
-            dst = wrap_in.at[pl.ds(pl.multiple_of(me_g * u, q), u)]
-            send(face_out.at[3, pl.ds(start, u)], dst, root_recv.at[0], (g, 0)).start()
+        start = pl.multiple_of((me_g & 1) * h, q)
+        dst = wrap_in.at[pl.ds(pl.multiple_of(me_g * u, q), u)]
+        send(face_out.at[3, pl.ds(start, u)], dst, root_recv, (root, 0)).start()
+
+    def wrap_target(a):
+        return lax.rem(me_g + (a + ng), ng)
+
+    def give_wrap(first):
+        for turn, a in ((2, 1), (0, -1), (1, 0)):
+            target = wrap_target(a)
+            wanted = target == 0 if first else (target != 0) & (target != root)
+
+            @pl.when(is_last & wanted)
+            def _():
+                send(j_out(3, 1), j_in(3, 1, turn), last_recv.at[3], (target, 0)).start()
+
+    give_wrap(True)
 
     @pl.when(is_near)
     def _():
-        for g in range(ng):
-            send(j_out(3, 1), slot(root_in, 2, me_g), root_recv.at[1], (g, 0)).start()
+        send(j_out(3, 1), slot(root_in, 2, me_g), root_recv, (root, 0)).start()
 
     give_i(3, [last_recv.at[0], last_recv.at[1]])
     give_j(3, 0, -1, last_recv.at[2])
@@ -387,17 +466,23 @@
     def _():
         give_j(3, 1, 1, last_recv.at[3])
 
-    @pl.when(is_first)
-    def _():
-        for a in range(1, ng):
-            send(j_out(3, 0), slot(root_in, 0, me_g), root_recv.at[1], at(a, 0)).start()
+    @pl.when(is_first & (me_g != root))
+    def _():
+        send(j_out(3, 0), slot(root_in, 0, me_g), root_recv, (root, 0)).start()
+
+    inside = assemble_inside(local, ez)
 
     @pl.when(jnp.logical_not(is_last))
     def _():
-        drain(2 * h + 3 * q, side_recv.at[0])
-
-    drain(3 * q, side_recv.at[1])
-    inverse = [1.0 / x for x in assembled(1, diag)]
+        gather_sides()
+
+    drain(6 * q, side_recv.at[1])
+    inverse = add_j_face([early_v[0, rows - ez :, c] for c in cut], ez, *turns(1, 0), 1)
+    inverse = [1.0 / x for x in inverse]
+    if rows > ez:
+        kept = slice(0, rows - ez)
+        inverse = [jnp.concatenate([early_v[2, kept, cut[b]], inverse[b]], axis=0) for b in range(4)]
+    mixed = [early_v[1, :, c] for c in cut]
 
     @pl.when(is_first)
     def _():
@@ -405,15 +490,37 @@
         ends = ((lane & 7) == 0) | ((lane & 7) == 7)
         share = jnp.where((lane < 64) & ((lane & 31) < 8), 0.0, jnp.where(ends, 0.5, 1.0))
         side_out[pl.ds(0, q)] = share * pack_j_face(inverse, ez, 0)
-        for a in range(1, ng):
-            send(side_out.at[pl.ds(0, q)], slot(root_in, 1, me_g), root_recv.at[1], at(a, 0)).start()
-
-    drain(span, recv_sem.at[1])
-    dual = assembled(2, mixed)
+
+    @pl.when(is_first & (me_g != root))
+    def _():
+        send(side_out.at[pl.ds(0, q)], slot(root_in, 1, me_g), root_recv, (root, 0)).start()
+
+    dual = add_j_face(mixed, ez, *turns(2, 0), 1)
     norm_now = total_of([spread_res[b] * residual[b] * inverse[b] for b in range(4)])
     curvature = total_of([smooth[b] * local[b] for b in range(4)])
     cross = total_of([local[b] * dual[b] * inverse[b] for b in range(4)])
     share = [owned[b] * inverse[b] for b in range(4)]
+    order = sorted(range(len(others)), key=lambda n: (others[n][1] != 1, others[n][1] != 0))
+
+    def tell(row, table, sem, which=None):
+        for n in order:
+            a, b = others[n]
+            if which is not None and which != (b == 1):
+                continue
+            send(part.at[pl.ds(row, 1)], table.at[pl.ds(n, 1)], sem, at(a, b)).start()
+
+    lane = lane_of((1, LANES))
+    early = jnp.where(lane < 32, norm_now, jnp.where(lane < 64, curvature, cross))
+    part[pl.ds(0, 1)] = early
+
+    @pl.when(jnp.logical_not(is_last))
+    def _():
+        tell(0, sums, sum_recv)
+
+    @pl.when(is_last)
+    def _():
+        tell(0, sums, sum_recv, True)
+
 
     def hold(ref, side):
         for n, value in enumerate(turns(3, side)):
@@ -427,7 +534,7 @@
         drain(h, last_recv.at[0])
         high_v[...] = i_in(3, 0)[...]
 
-    @pl.when(jnp.logical_not(owns_high))
+    @pl.when(is_last)
     def _():
         high_v[...] = jnp.zeros_like(high_v)
 
@@ -451,24 +558,36 @@
 
     mostly = add_i_face(inside, high_v[...], 1)
     mostly = add_j_face(add_j_face(mostly, ez, *held(prev_v), 0), ez, *held(next_v), 1)
-    quad = total_of([share[b] * mostly[b] * mostly[b] for b in range(4)])
-
-    lane = lane_of((1, LANES))
-    mine = jnp.where(
-        lane < 32, norm_now, jnp.where(lane < 64, curvature, jnp.where(lane < 96, cross, quad))
-    )
-    part[0] = mine
-    order = sorted(range(len(others)), key=lambda n: (others[n][1] != 0, others[n][1] != 1))
-    for n in order:
-        a, b = others[n]
-        send(part.at[0], parts.at[n], part_recv, at(a, b)).start()
-
-    @pl.when(is_first)
+    quad = stack([share[b] * mostly[b] * mostly[b] for b in range(4)])
+    quad = jnp.sum(quad, axis=0, keepdims=True)
+    part[pl.ds(1, 1)] = quad
+
+    @pl.when(owns_low)
+    def _():
+        face = pack_i_face(mostly[0], 0)
+        fit = pack_i_face(face_owned * inverse[0], 0)
+        drain(h, last_recv.at[1])
+        met = i_in(3, 1)[...]
+        low_v[...] = met
+        face = face + met
+        part[pl.ds(1, 1)] = quad + jnp.sum(face * face * fit, axis=0, keepdims=True)
+
+    @pl.when(jnp.logical_not(is_last))
+    def _():
+        tell(1, parts, part_recv)
+
+    @pl.when(is_last)
+    def _():
+        tell(1, parts, part_recv)
+        tell(0, sums, sum_recv, False)
+
+    give_wrap(False)
+
+    @pl.when(is_root)
     def _():
         slot(root_in, 0, me_g)[...] = j_out(3, 0)[...]
         slot(root_in, 1, me_g)[...] = side_out[pl.ds(0, q)]
-        drain((3 * ng - 2) * q + ng // 2 * h, root_recv.at[1])
-        drain(ng * u, root_recv.at[0])
+        drain((3 * ng - 2) * q + ng // 2 * h + ng * u, root_recv)
 
         def far(g):
             return wrap_in[pl.ds(u * g + (0 if g & 1 else h), q)]
@@ -498,24 +617,26 @@
             term = face * face * side_in[pl.ds(h * (g // 2), h)]
             for n in range(0, h, q):
                 total = total + term[n : n + q]
-        total = jnp.sum(jnp.sum(total, axis=0, keepdims=True), axis=1, keepdims=True)
-        late[0] = jnp.broadcast_to(total, (1, LANES))
-        late_out[0] = jnp.broadcast_to(total, (1, LANES))
+        total = jnp.sum(total, axis=0, keepdims=True)
+        parts[pl.ds(len(others), 1)] = total
+        late_out[...] = total
         for n, shift in enumerate((0, ng - 1, 1)):
             g = lax.rem(me_g + shift, ng)
             prev_v[pl.ds(q * n, q)] = wrap_in[pl.ds(pl.multiple_of(u * g + h * (1 - (g & 1)), q), q)]
 
-    speaks = is_first & odd
-
-    @pl.when(speaks)
-    def _():
-        for b in range(1, nd):
-            for a in (0, -1):
-                send(late_out.at[0], late.at[0], root_recv.at[2], at(a, b)).start()
-
-    drain(h, last_recv.at[1])
-
-    @pl.when(jnp.logical_not(owns_high))
+    heard = [(g, b) for b in range(nd) for g in range(ng) if (g, b) != (root, 0)]
+
+    @pl.when(is_root)
+    def _():
+        for target in heard:
+            send(late_out, parts.at[pl.ds(len(others), 1)], part_recv, target).start()
+
+    @pl.when(jnp.logical_not(owns_low))
+    def _():
+        drain(h, last_recv.at[1])
+        low_v[...] = i_in(3, 1)[...]
+
+    @pl.when(is_last)
     def _():
         drain(h, last_recv.at[0])
         high_v[...] = i_in(3, 0)[...]
@@ -525,39 +646,52 @@
         drain(3 * q, last_recv.at[2])
         hold(next_v, 0)
 
-    @pl.when(jnp.logical_not(is_last | is_first))
+    @pl.when(jnp.logical_not(is_last | is_root))
     def _():
         drain(3 * q, last_recv.at[3])
         hold(prev_v, 1)
 
-    applied = add_i_face(add_i_face(inside, high_v[...], 1), i_in(3, 1)[...], 0)
+    applied = add_i_face(add_i_face(inside, low_v[...], 0), high_v[...], 1)
     applied = add_j_face(add_j_face(applied, ez, *held(prev_v), 0), ez, *held(next_v), 1)
 
-    @pl.when(jnp.logical_not(is_first))
-    def _():
-        pltpu.make_async_copy(late, late, root_recv.at[2]).wait()
-
-    pltpu.make_async_copy(parts, parts, part_recv).wait()
-    everyone = mine + jnp.sum(parts[...], axis=0)
-    norm_now, curvature, cross, quad = (everyone[:, 32 * n : 32 * n + 1] for n in range(4))
-    quad = quad + late[0][:, :1]
+    drain(len(others), sum_recv)
+    everyone = early + jnp.sum(sums[pl.ds(0, len(others))], axis=0, keepdims=True)
+    norm_now, curvature, cross = (everyone[:, 32 * n : 32 * n + 1] for n in range(3))
     step = norm_now / curvature
-    norm_next = norm_now - 2.0 * step * cross + step * step * quad
-    ratio = norm_next / norm_now
+    shrunk = norm_now - 2.0 * step * cross
+    scale = step * step
+    moved = []
     for b, c in enumerate(cut):
         outs[0, :, c] = pair_v[1, :, c] + step * smooth[b]
         out = residual[b] - step * applied[b]
         outs[1, :, c] = out
-        outs[2, :, c] = out * inverse[b] + ratio * smooth[b]
-    common = 4 * span + len(others)
+        moved.append(out * inverse[b])
+
+    @pl.when(is_root)
+    def _():
+        drain(len(others), part_recv)
+
+    @pl.when(jnp.logical_not(is_root))
+    def _():
+        drain(len(others) + 1, part_recv)
+
+    quad = part[pl.ds(1, 1)] + jnp.sum(parts[...], axis=0, keepdims=True)
+    quad = jnp.sum(quad, axis=1, keepdims=True)
+    ratio = (shrunk + scale * quad) / norm_now
+    for b, c in enumerate(cut):
+        outs[2, :, c] = moved[b] + ratio * smooth[b]
+    common = 4 * span + 2 * len(others)
     roles = [
-        (is_first & odd, 2 * (ng - 1) * q + 2 * (nd - 1)),
-        (is_first & jnp.logical_not(odd), 2 * (ng - 1) * q),
-        (is_last & odd, ng * (u + h) - 3 * q),
-        (is_last & jnp.logical_not(odd), ng * u - 3 * q),
-        (is_near, ng * q),
+        (is_root, len(heard)),
+        (is_first & jnp.logical_not(is_root), 2 * q),
+        (is_near, q),
         (jnp.logical_not(is_first | is_last | is_near), 0),
     ]
+    skipped = sum(jnp.where(wrap_target(a) == root, 1, 0) for a in (-1, 0, 1))
+    for n in range(4):
+        roles.append((is_last & odd & (skipped == n), u + h - n * q))
+        roles.append((is_last & jnp.logical_not(odd) & (skipped == n), u - n * q))
+
     for role, extra in roles:
 
         @pl.when(role)
@@ -581,7 +715,8 @@
     table = jnp.asarray(tables())
     h, q = rows // 2, ez // 2
     u, q8 = h + q, 8
-    spare = 4 * (2 * h + 6 * q) + ng * nd + 2 * nd + ng * (u + h)
+    spare = 4 * (2 * h + 6 * q) + 2 * ng * nd + 3 * ng * (u + h)
+    bulk = (2 * rows * points * 4 + 4 * rows * points * 2 + table.size * 2) // (4 * LANES)
     spare = -(-spare // q8) * q8
     stacked = pl.pallas_call(
         functools.partial(kernel, ng, nd, ez),
@@ -593,6 +728,7 @@
             pltpu.VMEM(flat, f32),
             pltpu.VMEM((4,) + flat, bf16),
             pltpu.VMEM(table.shape, bf16),
+            pltpu.VMEM((3,) + flat, f32),
             pltpu.VMEM((4, 2 * u, LANES), f32),
             pltpu.VMEM((spare, LANES), f32),
             pltpu.VMEM((ng * u, LANES), f32),
@@ -602,16 +738,19 @@
             pltpu.VMEM((3 * q, LANES), f32),
             pltpu.VMEM((3 * q, LANES), f32),
             pltpu.VMEM((h, LANES), f32),
-            pltpu.VMEM((1, 1, LANES), f32),
-            pltpu.VMEM((ng * nd - 1, 1, LANES), f32),
-            pltpu.VMEM((1, 1, LANES), f32),
-            pltpu.VMEM((1, 1, LANES), f32),
+            pltpu.VMEM((h, LANES), f32),
+            pltpu.VMEM((2, LANES), f32),
+            pltpu.VMEM((ng * nd, LANES), f32),
+            pltpu.VMEM((ng * nd, LANES), f32),
+            pltpu.VMEM((1, LANES), f32),
+            pltpu.VMEM((bulk, LANES), f32),
+            pltpu.SemaphoreType.DMA((2,)),
+            pltpu.SemaphoreType.DMA,
+            pltpu.SemaphoreType.DMA,
+            pltpu.SemaphoreType.DMA((2,)),
             pltpu.SemaphoreType.DMA((4,)),
             pltpu.SemaphoreType.DMA,
-            pltpu.SemaphoreType.DMA((2,)),
-            pltpu.SemaphoreType.DMA((2,)),
-            pltpu.SemaphoreType.DMA((4,)),
-            pltpu.SemaphoreType.DMA((3,)),
+            pltpu.SemaphoreType.DMA,
             pltpu.SemaphoreType.DMA,
             pltpu.SemaphoreType.REGULAR,
         ],

time: 18.7 us -> 18.4 us (0.984)
  Pallas kernels: 17.9 us -> 17.7 us
    pallas_call x1, Pallas kernels: 17.3 us -> 17 us  [on_device(): pl.pallas_call(functools.partial(kernel, ng, nd, ez), out_shape=pltpu.VME...]
where the time goes in v4:
time: 18.4 us; the launch traced here: 18.3 us
  Pallas kernels  17.7 us (96%)
  between operations  0.64 us (3%)
    pallas_call x1, Pallas kernels, on_device(): pl.pallas_call(functools.partial(kernel, ng, nd, ez), out_shape=pltpu.VME...  17 us
    pallas_call x1, Pallas kernels, on_device(): pl.pallas_call(deliver, out_shape=[jax.ShapeDtypeStruct(flat, f32)] * 3,...  0.68 us

profile of v4, /device:TPU:0, one launch (start us, length us, event | category | flops | bytes accessed | tf_op | source)
XLA Modules:
  0.0 18.3 jit_solution(13769681164423913885)
XLA Ops:
  0.6 17.0 %shard_map.85.stacked = f32[3,32,512]{2,1,0:T(8,128)S(1)} custom-call(f32[32,512]{1,0:T(8,128)} %bitcast.9, f32[32,512]{1,0:T(8,128)} %bitcast.10, f32[32,512]{1,0:T(8,128)} %bitcast.11, bf16[3,32,512]{2,1,0:T(8,128)(2,1)} %bitcast.8, bf16[32,512]{1,0:T(8,128)(2,1)} %bitcast.12, bf16[256,1024]{1,0:T(8,128)(2,1)} %constant.2.clone.tab_h), custom_call_target="tpu_custom_call" | custom-call | tf_op jit(solution)/shard_map/pallas_call | solution.py:721
  17.6 0.7 %shard_map.86 = (f32[32,512]{1,0:T(8,128)}, f32[32,512]{1,0:T(8,128)}, f32[32,512]{1,0:T(8,128)}) custom-call(f32[3,32,512]{2,1,0:T(8,128)S(1)} %shard_map.85.stacked), custom_call_target="tpu_custom_call" | custom-call | tf_op jit(solution)/shard_map/pallas_call | solution.py:766

commit v5 on v4

--- a/solution.py
+++ b/solution.py
@@ -251,8 +251,8 @@
     sol_h, res_h, dir_h, geo_h, mass_h, tab_h,
     outs,
     pair_v, dir_v, geo_v, tab_v, early_v,
-    face_out, face_in, wrap_in, root_in, side_in, side_out, prev_v, next_v, low_v, high_v, part, sums, parts, late_out,
-    bulk, load_sem, send_sem, recv_sem, side_recv, last_recv, root_recv, sum_recv, part_recv, go,
+    face_out, face_in, wrap_in, root_in, relay_in, side_in, side_out, prev_v, next_v, low_v, high_v, part, sums, parts, late_out,
+    bulk, load_sem, send_sem, recv_sem, side_recv, last_recv, root_recv, relay_recv, sum_recv, part_recv, go,
 ):
     me_g, me_d = lax.axis_index("group"), lax.axis_index("dev")
 
@@ -269,13 +269,35 @@
     loads = [pltpu.make_async_copy(h, v, load_sem.at[n]) for h, v, n in pairs]
     loads[0].start()
     barrier = pltpu.get_barrier_semaphore()
+    is_first, is_last, is_near = me_d == 0, me_d == nd - 1, me_d == nd - 2
+    odd = (me_g & 1) == 1
+    is_relay = (me_d == nd - 3) & odd
+    own_relay = (me_g | 1, nd - 3)
     partners = [t for t in others if min(t[0], ng - t[0]) < 2 and min(t[1], nd - t[1]) < 2]
     hub = (1 % ng, nd // 2)
     hub_a, hub_b = lax.rem(me_g - hub[0] + ng, ng), lax.rem(me_d - hub[1] + nd, nd)
     at_hub = (hub_a == 0) & (hub_b == 0)
     near_hub = ((hub_a < 2) | (hub_a == ng - 1)) & ((hub_b < 2) | (hub_b == nd - 1))
+    @pl.when(is_last)
+    def _():
+        beside = lax.rem(jnp.where(odd, me_g + 2, me_g + (ng - 1)), ng)
+        for target in ((beside, nd - 3), own_relay):
+            pl.semaphore_signal(barrier, inc=1, device_id=target, device_id_type=MESH)
+
+    @pl.when(is_relay)
+    def _():
+        for target in ((me_g, 0), (me_g - 1, 0)):
+            pl.semaphore_signal(barrier, inc=1, device_id=target, device_id_type=MESH)
+
     for a, b in partners:
-        pl.semaphore_signal(barrier, inc=1, device_id=at(a, b), device_id_type=MESH)
+        if b == 1:
+
+            @pl.when(jnp.logical_not(is_last))
+            def _():
+                pl.semaphore_signal(barrier, inc=1, device_id=at(a, b), device_id_type=MESH)
+
+        else:
+            pl.semaphore_signal(barrier, inc=1, device_id=at(a, b), device_id_type=MESH)
 
     @pl.when(jnp.logical_not(near_hub))
     def _():
@@ -287,11 +309,9 @@
     rows = dir_v.shape[0]
     h, q = rows // 2, ez // 2
     u, span = h + q, 2 * h + 6 * q
-    is_first, is_last, is_near = me_d == 0, me_d == nd - 1, me_d == nd - 2
     root = min(1, ng - 1)
     is_root = is_first & (me_g == root)
-    odd = (me_g & 1) == 1
-    owns_next = me_d < nd - 2
+    owns_next = me_d < nd - 3
     owns_high, owns_low = jnp.logical_not(is_last), is_last & odd
 
     def i_out(phase, side):
@@ -335,10 +355,13 @@
         for side, step in ((0, -1), (1, 1)):
             send(i_out(phase, side), i_in(phase, side), sems[side], at(step, 0)).start()
 
-    def give(phase, sems):
-        give_j(phase, 0, -1, sems[2])
-        give_j(phase, 1, 1, sems[3])
+    def give_rest(phase, sems):
+        give_j(phase, 1, 1, sems[2])
         give_i(phase, sems[:2])
+
+    def give_relay(phase, sem):
+        dst = relay_in.at[pl.ds(pl.multiple_of(q * (2 * phase + (me_g & 1)), q), q)]
+        send(j_out(phase, 0), dst, sem, own_relay).start()
 
     def turns(phase, side):
         return [j_in(phase, side, turn)[...] for turn in (1, 2, 0)]
@@ -351,8 +374,14 @@
     loads[0].wait()
     weighted = assemble_inside([weights[b] * dir_v[:, cut[b]] for b in range(4)], ez)
     pack(0, weighted)
-    pl.semaphore_wait(barrier, jnp.where(at_hub, len(others), len(partners)))
-    give(0, [recv_sem] * 4)
+    count = jnp.where(at_hub, len(others), len(partners))
+    count = jnp.where(is_relay, len(partners) + 4, count)
+
+    @pl.when(jnp.logical_not(is_first))
+    def _():
+        pl.semaphore_wait(barrier, count)
+        give_j(0, 0, -1, recv_sem)
+        give_rest(0, [recv_sem] * 3)
 
     @pl.when(at_hub)
     def _():
@@ -369,13 +398,43 @@
     diag = [diag[b] + squared[rows * b : rows * b + rows] + mass[b] for b in range(4)]
     diag = assemble_inside(diag, ez)
     pack(1, diag)
-    give(1, [side_recv.at[0], side_recv.at[0], side_recv.at[1], side_recv.at[0]])
     residual = [pair_v[0, :, c] for c in cut]
     spread_res = [weights[b] * residual[b] for b in range(4)]
     mixed = assemble_inside(spread_res, ez)
     pack(2, mixed)
-    give(2, [side_recv.at[0], side_recv.at[0], side_recv.at[1], side_recv.at[0]])
-    owned, face_owned = owner_weights(rows, ez, is_last, owns_next, owns_high)
+
+    @pl.when(is_first)
+    def _():
+        pl.semaphore_wait(barrier, len(partners) - 2)
+        give_relay(0, relay_recv.at[me_g & 1])
+        give_relay(1, relay_recv.at[2])
+        give_relay(2, relay_recv.at[2])
+        give_rest(0, [recv_sem] * 3)
+
+    @pl.when(jnp.logical_not(is_first))
+    def _():
+        give_j(1, 0, -1, side_recv.at[1])
+        give_j(2, 0, -1, side_recv.at[1])
+
+    give_rest(1, [side_recv.at[0]] * 3)
+    give_rest(2, [side_recv.at[0]] * 3)
+    owned, face_owned = owner_weights(rows, ez, False, owns_next, owns_high)
+
+    def pass_on(phase, core, sem):
+        for turn, a in ((2, 1), (0, -1), (1, 0)):
+            target = lax.rem(me_g + (core - 1 + a + ng), ng)
+            src = relay_in.at[pl.ds(q * (2 * phase + core), q)]
+            send(src, j_in(phase, 0, turn), sem, (target, nd - 1)).start()
+
+    @pl.when(is_relay)
+    def _():
+        for core in (1, 0):
+            drain(q, relay_recv.at[core])
+            pass_on(0, core, recv_sem)
+        drain(4 * q, relay_recv.at[2])
+        for phase in (1, 2):
+            for core in (1, 0):
+                pass_on(phase, core, side_recv.at[1])
 
     @pl.when(jnp.logical_not(at_hub))
     def _():
@@ -406,7 +465,7 @@
         lane = lane_of((h, LANES))
         row = lax.broadcasted_iota(jnp.int32, (h, LANES), 0) + jnp.where(lane < 64, 0, h)
         j, k = (lane >> 3) & 7, lane & 7
-        fit = jnp.where(j == 0, jnp.where(row < ez, 1.0, 0.5), 1.0)
+        fit = jnp.where(j == 0, jnp.where(row < ez, 0.0, 0.5), 1.0)
         fit = jnp.where(j == 7, jnp.where(row < rows - ez, 0.5, 0.0), fit)
         fit = fit * jnp.where((k == 0) | (k == 7), 0.5, 1.0)
         side_out[...] = fit * pack_i_face(early_v[2, :, cut[3]], 1)
@@ -453,11 +512,20 @@
             def _():
                 send(j_out(3, 1), j_in(3, 1, turn), last_recv.at[3], (target, 0)).start()
 
+    @pl.when(is_last)
+    def _():
+        send(j_out(3, 0), slot(root_in, 5, me_g), root_recv, (root, 0)).start()
+
     give_wrap(True)
 
     @pl.when(is_near)
     def _():
         send(j_out(3, 1), slot(root_in, 2, me_g), root_recv, (root, 0)).start()
+        send(j_out(3, 0), slot(root_in, 3, me_g), root_recv, (root, 0)).start()
+
+    @pl.when(me_d == nd - 3)
+    def _():
+        send(j_out(3, 1), slot(root_in, 4, me_g), root_recv, (root, 0)).start()
 
     give_i(3, [last_recv.at[0], last_recv.at[1]])
     give_j(3, 0, -1, last_recv.at[2])
@@ -484,16 +552,25 @@
         inverse = [jnp.concatenate([early_v[2, kept, cut[b]], inverse[b]], axis=0) for b in range(4)]
     mixed = [early_v[1, :, c] for c in cut]
 
-    @pl.when(is_first)
-    def _():
+    def shared(side):
         lane = lane_of((q, LANES))
         ends = ((lane & 7) == 0) | ((lane & 7) == 7)
         share = jnp.where((lane < 64) & ((lane & 31) < 8), 0.0, jnp.where(ends, 0.5, 1.0))
-        side_out[pl.ds(0, q)] = share * pack_j_face(inverse, ez, 0)
+        return share * pack_j_face(inverse, ez, side)
+
+    @pl.when(is_first | is_near)
+    def _():
+        side_out[pl.ds(0, q)] = shared(0)
 
     @pl.when(is_first & (me_g != root))
     def _():
         send(side_out.at[pl.ds(0, q)], slot(root_in, 1, me_g), root_recv, (root, 0)).start()
+
+    @pl.when(is_near)
+    def _():
+        side_out[pl.ds(q, q)] = shared(1)
+        dst = root_in.at[pl.ds(pl.multiple_of(q * (6 * ng + 2 * me_g), q), 2 * q)]
+        send(side_out.at[pl.ds(0, 2 * q)], dst, root_recv, (root, 0)).start()
 
     dual = add_j_face(mixed, ez, *turns(2, 0), 1)
     norm_now = total_of([spread_res[b] * residual[b] * inverse[b] for b in range(4)])
@@ -547,17 +624,8 @@
     def _():
         next_v[...] = jnp.zeros_like(next_v)
 
-    @pl.when(is_last)
-    def _():
-        drain(3 * q, last_recv.at[3])
-        hold(prev_v, 1)
-
-    @pl.when(jnp.logical_not(is_last))
-    def _():
-        prev_v[...] = jnp.zeros_like(prev_v)
-
     mostly = add_i_face(inside, high_v[...], 1)
-    mostly = add_j_face(add_j_face(mostly, ez, *held(prev_v), 0), ez, *held(next_v), 1)
+    mostly = add_j_face(mostly, ez, *held(next_v), 1)
     quad = stack([share[b] * mostly[b] * mostly[b] for b in range(4)])
     quad = jnp.sum(quad, axis=0, keepdims=True)
     part[pl.ds(1, 1)] = quad
@@ -587,7 +655,7 @@
     def _():
         slot(root_in, 0, me_g)[...] = j_out(3, 0)[...]
         slot(root_in, 1, me_g)[...] = side_out[pl.ds(0, q)]
-        drain((3 * ng - 2) * q + ng // 2 * h + ng * u, root_recv)
+        drain((8 * ng - 2) * q + ng // 2 * h + ng * u, root_recv)
 
         def far(g):
             return wrap_in[pl.ds(u * g + (0 if g & 1 else h), q)]
@@ -595,25 +663,28 @@
         def across(g):
             return wrap_in[pl.ds(u * g + (q if g & 1 else 0), h)]
 
-        def near(g):
-            return root_in[pl.ds(q * (2 * ng + g), q)]
+        def got(part_of, g):
+            return root_in[pl.ds(q * (ng * part_of + g), q)]
+
+        def paired(g, n):
+            return root_in[pl.ds(q * (6 * ng + 2 * g + n), q)]
 
         spot = lane_of((q, LANES))
         seam = (spot >= 64) & ((spot & 31) >= 24)
-        faces = [far(g) + root_in[pl.ds(q * g, q)] for g in range(ng)]
         total = None
-        for g in range(ng):
-            face = faces[g] + jnp.where(seam, roll(faces[(g + 1) % ng], 88), 0.0)
-            term = face * face * root_in[pl.ds(q * (ng + g), q)]
-            total = term if total is None else total + term
-        spot = lane_of((ez, LANES))
+        groups = range(ng)
+        seams = (
+            ([got(3, g) + got(4, g) for g in groups], [paired(g, 0) for g in groups]),
+            ([got(2, g) + got(5, g) for g in groups], [paired(g, 1) for g in groups]),
+            ([got(0, g) + far(g) for g in groups], [got(1, g) for g in groups]),
+        )
+        for faces, fits in seams:
+            for g in groups:
+                face = faces[g] + jnp.where(seam, roll(faces[(g + 1) % ng], 88), 0.0)
+                term = face * face * fits[g]
+                total = term if total is None else total + term
         for g in range(1, ng, 2):
-            one, two = near(g), near((g + 1) % ng)
-            line = jnp.concatenate([roll(one, -88) + two, roll(one, -120) + roll(two, -32)], axis=0)
-            line = jnp.where(spot < 8, line, 0.0)
-            if h > ez:
-                line = jnp.concatenate([line, jnp.zeros((h - ez, LANES), jnp.float32)], axis=0)
-            face = across(g) + across((g + 1) % ng) + line
+            face = across(g) + across((g + 1) % ng)
             term = face * face * side_in[pl.ds(h * (g // 2), h)]
             for n in range(0, h, q):
                 total = total + term[n : n + q]
@@ -646,7 +717,7 @@
         drain(3 * q, last_recv.at[2])
         hold(next_v, 0)
 
-    @pl.when(jnp.logical_not(is_last | is_root))
+    @pl.when(jnp.logical_not(is_root))
     def _():
         drain(3 * q, last_recv.at[3])
         hold(prev_v, 1)
@@ -682,15 +753,18 @@
         outs[2, :, c] = moved[b] + ratio * smooth[b]
     common = 4 * span + 2 * len(others)
     roles = [
-        (is_root, len(heard)),
-        (is_first & jnp.logical_not(is_root), 2 * q),
-        (is_near, q),
-        (jnp.logical_not(is_first | is_last | is_near), 0),
+        (is_root, len(heard) - 6 * q),
+        (is_first & jnp.logical_not(is_root), 2 * q - 6 * q),
+        (is_near, 4 * q),
+        (is_relay, 19 * q),
+        ((me_d == nd - 3) & jnp.logical_not(odd), q),
+        (me_d * (nd - 4 - me_d) > 0, 0),
+        (me_d == nd - 4, 0),
     ]
     skipped = sum(jnp.where(wrap_target(a) == root, 1, 0) for a in (-1, 0, 1))
     for n in range(4):
-        roles.append((is_last & odd & (skipped == n), u + h - n * q))
-        roles.append((is_last & jnp.logical_not(odd) & (skipped == n), u - n * q))
+        roles.append((is_last & odd & (skipped == n), u + h + q - n * q))
+        roles.append((is_last & jnp.logical_not(odd) & (skipped == n), u + q - n * q))
 
     for role, extra in roles:
 
@@ -715,7 +789,7 @@
     table = jnp.asarray(tables())
     h, q = rows // 2, ez // 2
     u, q8 = h + q, 8
-    spare = 4 * (2 * h + 6 * q) + 2 * ng * nd + 3 * ng * (u + h)
+    spare = 4 * (2 * h + 6 * q) + 3 * ng * nd + 8 * ng * (u + h)
     bulk = (2 * rows * points * 4 + 4 * rows * points * 2 + table.size * 2) // (4 * LANES)
     spare = -(-spare // q8) * q8
     stacked = pl.pallas_call(
@@ -732,7 +806,8 @@
             pltpu.VMEM((4, 2 * u, LANES), f32),
             pltpu.VMEM((spare, LANES), f32),
             pltpu.VMEM((ng * u, LANES), f32),
-            pltpu.VMEM((3 * ng * q, LANES), f32),
+            pltpu.VMEM((8 * ng * q, LANES), f32),
+            pltpu.VMEM((6 * q, LANES), f32),
             pltpu.VMEM((ng // 2 * h, LANES), f32),
             pltpu.VMEM((h, LANES), f32),
             pltpu.VMEM((3 * q, LANES), f32),
@@ -750,6 +825,7 @@
             pltpu.SemaphoreType.DMA((2,)),
             pltpu.SemaphoreType.DMA((4,)),
             pltpu.SemaphoreType.DMA,
+            pltpu.SemaphoreType.DMA((3,)),
             pltpu.SemaphoreType.DMA,
             pltpu.SemaphoreType.DMA,
             pltpu.SemaphoreType.REGULAR,

time: 18.4 us -> 17.9 us (0.973)
  Pallas kernels: 17.7 us -> 17.1 us
    pallas_call x1, Pallas kernels: 17 us -> 16.4 us  [on_device(): pl.pallas_call(functools.partial(kernel, ng, nd, ez), out_shape=pltpu.VME...]
where the time goes in v5:
time: 17.9 us; the launch traced here: 17.7 us
  Pallas kernels  17.1 us (96%)
  between operations  0.64 us (4%)
    pallas_call x1, Pallas kernels, on_device(): pl.pallas_call(functools.partial(kernel, ng, nd, ez), out_shape=pltpu.VME...  16.4 us
    pallas_call x1, Pallas kernels, on_device(): pl.pallas_call(deliver, out_shape=[jax.ShapeDtypeStruct(flat, f32)] * 3,...  0.68 us

profile of v5, /device:TPU:0, one launch (start us, length us, event | category | flops | bytes accessed | tf_op | source)
XLA Modules:
  0.0 17.7 jit_solution(7395326828418641177)
XLA Ops:
  0.6 16.4 %shard_map.85.stacked = f32[3,32,512]{2,1,0:T(8,128)S(1)} custom-call(f32[32,512]{1,0:T(8,128)} %bitcast.9, f32[32,512]{1,0:T(8,128)} %bitcast.10, f32[32,512]{1,0:T(8,128)} %bitcast.11, bf16[3,32,512]{2,1,0:T(8,128)(2,1)} %bitcast.8, bf16[32,512]{1,0:T(8,128)(2,1)} %bitcast.12, bf16[256,1024]{1,0:T(8,128)(2,1)} %constant.2.clone.tab_h), custom_call_target="tpu_custom_call" | custom-call | tf_op jit(solution)/shard_map/pallas_call | solution.py:795
  17.1 0.7 %shard_map.86 = (f32[32,512]{1,0:T(8,128)}, f32[32,512]{1,0:T(8,128)}, f32[32,512]{1,0:T(8,128)}) custom-call(f32[3,32,512]{2,1,0:T(8,128)S(1)} %shard_map.85.stacked), custom_call_target="tpu_custom_call" | custom-call | tf_op jit(solution)/shard_map/pallas_call | solution.py:842

commit v6 on v5

--- a/solution.py
+++ b/solution.py
@@ -271,8 +271,9 @@
     barrier = pltpu.get_barrier_semaphore()
     is_first, is_last, is_near = me_d == 0, me_d == nd - 1, me_d == nd - 2
     odd = (me_g & 1) == 1
-    is_relay = (me_d == nd - 3) & odd
-    own_relay = (me_g | 1, nd - 3)
+    middle = nd // 2 - 1
+    is_relay = (me_d == middle) & odd
+    own_relay = (me_g | 1, middle)
     partners = [t for t in others if min(t[0], ng - t[0]) < 2 and min(t[1], nd - t[1]) < 2]
     hub = (1 % ng, nd // 2)
     hub_a, hub_b = lax.rem(me_g - hub[0] + ng, ng), lax.rem(me_d - hub[1] + nd, nd)
@@ -281,7 +282,7 @@
     @pl.when(is_last)
     def _():
         beside = lax.rem(jnp.where(odd, me_g + 2, me_g + (ng - 1)), ng)
-        for target in ((beside, nd - 3), own_relay):
+        for target in ((beside, middle), own_relay):
             pl.semaphore_signal(barrier, inc=1, device_id=target, device_id_type=MESH)
 
     @pl.when(is_relay)
@@ -311,7 +312,8 @@
     u, span = h + q, 2 * h + 6 * q
     root = min(1, ng - 1)
     is_root = is_first & (me_g == root)
-    owns_next = me_d < nd - 3
+    owns_next = me_d < nd - 5
+    is_mid = (me_d == nd - 3) | (me_d == nd - 4)
     owns_high, owns_low = jnp.logical_not(is_last), is_last & odd
 
     def i_out(phase, side):
@@ -523,9 +525,15 @@
         send(j_out(3, 1), slot(root_in, 2, me_g), root_recv, (root, 0)).start()
         send(j_out(3, 0), slot(root_in, 3, me_g), root_recv, (root, 0)).start()
 
-    @pl.when(me_d == nd - 3)
-    def _():
-        send(j_out(3, 1), slot(root_in, 4, me_g), root_recv, (root, 0)).start()
+    @pl.when(is_mid | (me_d == nd - 5))
+    def _():
+        where = jnp.where(me_d == nd - 3, 4, jnp.where(me_d == nd - 4, 8, 11))
+        send(j_out(3, 1), slot(root_in, where, me_g), root_recv, (root, 0)).start()
+
+    @pl.when(is_mid)
+    def _():
+        where = jnp.where(me_d == nd - 3, 9, 12)
+        send(j_out(3, 0), slot(root_in, where, me_g), root_recv, (root, 0)).start()
 
     give_i(3, [last_recv.at[0], last_recv.at[1]])
     give_j(3, 0, -1, last_recv.at[2])
@@ -558,9 +566,14 @@
         share = jnp.where((lane < 64) & ((lane & 31) < 8), 0.0, jnp.where(ends, 0.5, 1.0))
         return share * pack_j_face(inverse, ez, side)
 
-    @pl.when(is_first | is_near)
+    @pl.when(is_first | is_near | is_mid)
     def _():
         side_out[pl.ds(0, q)] = shared(0)
+
+    @pl.when(is_mid)
+    def _():
+        where = jnp.where(me_d == nd - 3, 10, 13)
+        send(side_out.at[pl.ds(0, q)], slot(root_in, where, me_g), root_recv, (root, 0)).start()
 
     @pl.when(is_first & (me_g != root))
     def _():
@@ -655,7 +668,7 @@
     def _():
         slot(root_in, 0, me_g)[...] = j_out(3, 0)[...]
         slot(root_in, 1, me_g)[...] = side_out[pl.ds(0, q)]
-        drain((8 * ng - 2) * q + ng // 2 * h + ng * u, root_recv)
+        drain((14 * ng - 2) * q + ng // 2 * h + ng * u, root_recv)
 
         def far(g):
             return wrap_in[pl.ds(u * g + (0 if g & 1 else h), q)]
@@ -676,6 +689,8 @@
         seams = (
             ([got(3, g) + got(4, g) for g in groups], [paired(g, 0) for g in groups]),
             ([got(2, g) + got(5, g) for g in groups], [paired(g, 1) for g in groups]),
+            ([got(8, g) + got(9, g) for g in groups], [got(10, g) for g in groups]),
+            ([got(11, g) + got(12, g) for g in groups], [got(13, g) for g in groups]),
             ([got(0, g) + far(g) for g in groups], [got(1, g) for g in groups]),
         )
         for faces, fits in seams:
@@ -756,10 +771,11 @@
         (is_root, len(heard) - 6 * q),
         (is_first & jnp.logical_not(is_root), 2 * q - 6 * q),
         (is_near, 4 * q),
-        (is_relay, 19 * q),
-        ((me_d == nd - 3) & jnp.logical_not(odd), q),
-        (me_d * (nd - 4 - me_d) > 0, 0),
-        (me_d == nd - 4, 0),
+        (is_mid, 3 * q),
+        ((me_d == nd - 5) & is_relay, 19 * q),
+        ((me_d == nd - 5) & jnp.logical_not(is_relay), q),
+        ((me_d > 0) & (me_d < nd - 5) & is_relay, 18 * q),
+        ((me_d > 0) & (me_d < nd - 5) & jnp.logical_not(is_relay), 0),
     ]
     skipped = sum(jnp.where(wrap_target(a) == root, 1, 0) for a in (-1, 0, 1))
     for n in range(4):
@@ -789,7 +805,7 @@
     table = jnp.asarray(tables())
     h, q = rows // 2, ez // 2
     u, q8 = h + q, 8
-    spare = 4 * (2 * h + 6 * q) + 3 * ng * nd + 8 * ng * (u + h)
+    spare = max(14 * ng * q + ng * (u + h), 4 * (2 * h + 6 * q) + 3 * ng * nd + 32 * q)
     bulk = (2 * rows * points * 4 + 4 * rows * points * 2 + table.size * 2) // (4 * LANES)
     spare = -(-spare // q8) * q8
     stacked = pl.pallas_call(
@@ -806,7 +822,7 @@
             pltpu.VMEM((4, 2 * u, LANES), f32),
             pltpu.VMEM((spare, LANES), f32),
             pltpu.VMEM((ng * u, LANES), f32),
-            pltpu.VMEM((8 * ng * q, LANES), f32),
+            pltpu.VMEM((14 * ng * q, LANES), f32),
             pltpu.VMEM((6 * q, LANES), f32),
             pltpu.VMEM((ng // 2 * h, LANES), f32),
             pltpu.VMEM((h, LANES), f32),

time: 17.9 us -> 17.5 us (0.978)
  Pallas kernels: 17.1 us -> 16.7 us
    pallas_call x1, Pallas kernels: 16.4 us -> 16 us  [on_device(): pl.pallas_call(functools.partial(kernel, ng, nd, ez), out_shape=pltpu.VME...]
where the time goes in v6:
time: 17.5 us; the launch traced here: 17.3 us
  Pallas kernels  16.7 us (95%)
  between operations  0.64 us (4%)
    pallas_call x1, Pallas kernels, on_device(): pl.pallas_call(functools.partial(kernel, ng, nd, ez), out_shape=pltpu.VME...  16 us
    pallas_call x1, Pallas kernels, on_device(): pl.pallas_call(deliver, out_shape=[jax.ShapeDtypeStruct(flat, f32)] * 3,...  0.68 us

profile of v6, /device:TPU:0, one launch (start us, length us, event | category | flops | bytes accessed | tf_op | source)
XLA Modules:
  0.0 17.3 jit_solution(9516738544877255996)
XLA Ops:
  0.6 16.0 %shard_map.85.stacked = f32[3,32,512]{2,1,0:T(8,128)S(1)} custom-call(f32[32,512]{1,0:T(8,128)} %bitcast.9, f32[32,512]{1,0:T(8,128)} %bitcast.10, f32[32,512]{1,0:T(8,128)} %bitcast.11, bf16[3,32,512]{2,1,0:T(8,128)(2,1)} %bitcast.8, bf16[32,512]{1,0:T(8,128)(2,1)} %bitcast.12, bf16[256,1024]{1,0:T(8,128)(2,1)} %constant.2.clone.tab_h), custom_call_target="tpu_custom_call" | custom-call | tf_op jit(solution)/shard_map/pallas_call | solution.py:811
  16.6 0.7 %shard_map.86 = (f32[32,512]{1,0:T(8,128)}, f32[32,512]{1,0:T(8,128)}, f32[32,512]{1,0:T(8,128)}) custom-call(f32[3,32,512]{2,1,0:T(8,128)S(1)} %shard_map.85.stacked), custom_call_target="tpu_custom_call" | custom-call | tf_op jit(solution)/shard_map/pallas_call | solution.py:858

commit v7 on v6

--- a/solution.py
+++ b/solution.py
@@ -312,8 +312,9 @@
     u, span = h + q, 2 * h + 6 * q
     root = min(1, ng - 1)
     is_root = is_first & (me_g == root)
-    owns_next = me_d < nd - 5
-    is_mid = (me_d == nd - 3) | (me_d == nd - 4)
+    owns_next = me_d < nd - 7
+    is_mid = (me_d >= nd - 6) & (me_d <= nd - 3)
+    place = 3 * (nd - 3 - me_d)
     owns_high, owns_low = jnp.logical_not(is_last), is_last & odd
 
     def i_out(phase, side):
@@ -525,15 +526,14 @@
         send(j_out(3, 1), slot(root_in, 2, me_g), root_recv, (root, 0)).start()
         send(j_out(3, 0), slot(root_in, 3, me_g), root_recv, (root, 0)).start()
 
-    @pl.when(is_mid | (me_d == nd - 5))
-    def _():
-        where = jnp.where(me_d == nd - 3, 4, jnp.where(me_d == nd - 4, 8, 11))
+    @pl.when(is_mid | (me_d == nd - 7))
+    def _():
+        where = jnp.where(me_d == nd - 3, 4, 5 + place)
         send(j_out(3, 1), slot(root_in, where, me_g), root_recv, (root, 0)).start()
 
     @pl.when(is_mid)
     def _():
-        where = jnp.where(me_d == nd - 3, 9, 12)
-        send(j_out(3, 0), slot(root_in, where, me_g), root_recv, (root, 0)).start()
+        send(j_out(3, 0), slot(root_in, 9 + place, me_g), root_recv, (root, 0)).start()
 
     give_i(3, [last_recv.at[0], last_recv.at[1]])
     give_j(3, 0, -1, last_recv.at[2])
@@ -572,8 +572,7 @@
 
     @pl.when(is_mid)
     def _():
-        where = jnp.where(me_d == nd - 3, 10, 13)
-        send(side_out.at[pl.ds(0, q)], slot(root_in, where, me_g), root_recv, (root, 0)).start()
+        send(side_out.at[pl.ds(0, q)], slot(root_in, 10 + place, me_g), root_recv, (root, 0)).start()
 
     @pl.when(is_first & (me_g != root))
     def _():
@@ -668,7 +667,7 @@
     def _():
         slot(root_in, 0, me_g)[...] = j_out(3, 0)[...]
         slot(root_in, 1, me_g)[...] = side_out[pl.ds(0, q)]
-        drain((14 * ng - 2) * q + ng // 2 * h + ng * u, root_recv)
+        drain((20 * ng - 2) * q + ng // 2 * h + ng * u, root_recv)
 
         def far(g):
             return wrap_in[pl.ds(u * g + (0 if g & 1 else h), q)]
@@ -691,6 +690,8 @@
             ([got(2, g) + got(5, g) for g in groups], [paired(g, 1) for g in groups]),
             ([got(8, g) + got(9, g) for g in groups], [got(10, g) for g in groups]),
             ([got(11, g) + got(12, g) for g in groups], [got(13, g) for g in groups]),
+            ([got(14, g) + got(15, g) for g in groups], [got(16, g) for g in groups]),
+            ([got(17, g) + got(18, g) for g in groups], [got(19, g) for g in groups]),
             ([got(0, g) + far(g) for g in groups], [got(1, g) for g in groups]),
         )
         for faces, fits in seams:
@@ -771,11 +772,12 @@
         (is_root, len(heard) - 6 * q),
         (is_first & jnp.logical_not(is_root), 2 * q - 6 * q),
         (is_near, 4 * q),
-        (is_mid, 3 * q),
-        ((me_d == nd - 5) & is_relay, 19 * q),
-        ((me_d == nd - 5) & jnp.logical_not(is_relay), q),
-        ((me_d > 0) & (me_d < nd - 5) & is_relay, 18 * q),
-        ((me_d > 0) & (me_d < nd - 5) & jnp.logical_not(is_relay), 0),
+        (is_mid & is_relay, 21 * q),
+        (is_mid & jnp.logical_not(is_relay), 3 * q),
+        ((me_d == nd - 7) & is_relay, 19 * q),
+        ((me_d == nd - 7) & jnp.logical_not(is_relay), q),
+        ((me_d > 0) & (me_d < nd - 7) & is_relay, 18 * q),
+        ((me_d > 0) & (me_d < nd - 7) & jnp.logical_not(is_relay), 0),
     ]
     skipped = sum(jnp.where(wrap_target(a) == root, 1, 0) for a in (-1, 0, 1))
     for n in range(4):
@@ -805,7 +807,7 @@
     table = jnp.asarray(tables())
     h, q = rows // 2, ez // 2
     u, q8 = h + q, 8
-    spare = max(14 * ng * q + ng * (u + h), 4 * (2 * h + 6 * q) + 3 * ng * nd + 32 * q)
+    spare = max(20 * ng * q + ng * (u + h), 4 * (2 * h + 6 * q) + 3 * ng * nd + 32 * q)
     bulk = (2 * rows * points * 4 + 4 * rows * points * 2 + table.size * 2) // (4 * LANES)
     spare = -(-spare // q8) * q8
     stacked = pl.pallas_call(
@@ -822,7 +824,7 @@
             pltpu.VMEM((4, 2 * u, LANES), f32),
             pltpu.VMEM((spare, LANES), f32),
             pltpu.VMEM((ng * u, LANES), f32),
-            pltpu.VMEM((14 * ng * q, LANES), f32),
+            pltpu.VMEM((20 * ng * q, LANES), f32),
             pltpu.VMEM((6 * q, LANES), f32),
             pltpu.VMEM((ng // 2 * h, LANES), f32),
             pltpu.VMEM((h, LANES), f32),

time: 17.5 us -> 17.2 us (0.983)
  Pallas kernels: 16.7 us -> 16.4 us
    pallas_call x1, Pallas kernels: 16 us -> 15.7 us  [on_device(): pl.pallas_call(functools.partial(kernel, ng, nd, ez), out_shape=pltpu.VME...]
where the time goes in v7:
time: 17.2 us; the launch traced here: 17 us
  Pallas kernels  16.4 us (95%)
  between operations  0.64 us (4%)
    pallas_call x1, Pallas kernels, on_device(): pl.pallas_call(functools.partial(kernel, ng, nd, ez), out_shape=pltpu.VME...  15.7 us
    pallas_call x1, Pallas kernels, on_device(): pl.pallas_call(deliver, out_shape=[jax.ShapeDtypeStruct(flat, f32)] * 3,...  0.68 us

profile of v7, /device:TPU:0, one launch (start us, length us, event | category | flops | bytes accessed | tf_op | source)
XLA Modules:
  0.0 17.0 jit_solution(15049795104806533434)
XLA Ops:
  0.6 15.7 %shard_map.85.stacked = f32[3,32,512]{2,1,0:T(8,128)S(1)} custom-call(f32[32,512]{1,0:T(8,128)} %bitcast.9, f32[32,512]{1,0:T(8,128)} %bitcast.10, f32[32,512]{1,0:T(8,128)} %bitcast.11, bf16[3,32,512]{2,1,0:T(8,128)(2,1)} %bitcast.8, bf16[32,512]{1,0:T(8,128)(2,1)} %bitcast.12, bf16[256,1024]{1,0:T(8,128)(2,1)} %constant.2.clone.tab_h), custom_call_target="tpu_custom_call" | custom-call | tf_op jit(solution)/shard_map/pallas_call | solution.py:813
  16.4 0.7 %shard_map.86 = (f32[32,512]{1,0:T(8,128)}, f32[32,512]{1,0:T(8,128)}, f32[32,512]{1,0:T(8,128)}) custom-call(f32[3,32,512]{2,1,0:T(8,128)S(1)} %shard_map.85.stacked), custom_call_target="tpu_custom_call" | custom-call | tf_op jit(solution)/shard_map/pallas_call | solution.py:860

commit v8 on v7

--- a/solution.py
+++ b/solution.py
@@ -473,7 +473,7 @@
         fit = fit * jnp.where((k == 0) | (k == 7), 0.5, 1.0)
         side_out[...] = fit * pack_i_face(early_v[2, :, cut[3]], 1)
         dst = side_in.at[pl.ds(pl.multiple_of((me_g >> 1) * h, q), h)]
-        send(side_out, dst, root_recv, (root, 0)).start()
+        send(side_out, dst, root_recv.at[0], (root, 0)).start()
 
     drain(span, recv_sem)
     smooth = assembled(0, weighted)
@@ -501,7 +501,7 @@
     def _():
         start = pl.multiple_of((me_g & 1) * h, q)
         dst = wrap_in.at[pl.ds(pl.multiple_of(me_g * u, q), u)]
-        send(face_out.at[3, pl.ds(start, u)], dst, root_recv, (root, 0)).start()
+        send(face_out.at[3, pl.ds(start, u)], dst, root_recv.at[1], (root, 0)).start()
 
     def wrap_target(a):
         return lax.rem(me_g + (a + ng), ng)
@@ -517,23 +517,23 @@
 
     @pl.when(is_last)
     def _():
-        send(j_out(3, 0), slot(root_in, 5, me_g), root_recv, (root, 0)).start()
+        send(j_out(3, 0), slot(root_in, 5, me_g), root_recv.at[1], (root, 0)).start()
 
     give_wrap(True)
 
     @pl.when(is_near)
     def _():
-        send(j_out(3, 1), slot(root_in, 2, me_g), root_recv, (root, 0)).start()
-        send(j_out(3, 0), slot(root_in, 3, me_g), root_recv, (root, 0)).start()
+        send(j_out(3, 1), slot(root_in, 2, me_g), root_recv.at[0], (root, 0)).start()
+        send(j_out(3, 0), slot(root_in, 3, me_g), root_recv.at[0], (root, 0)).start()
 
     @pl.when(is_mid | (me_d == nd - 7))
     def _():
         where = jnp.where(me_d == nd - 3, 4, 5 + place)
-        send(j_out(3, 1), slot(root_in, where, me_g), root_recv, (root, 0)).start()
+        send(j_out(3, 1), slot(root_in, where, me_g), root_recv.at[0], (root, 0)).start()
 
     @pl.when(is_mid)
     def _():
-        send(j_out(3, 0), slot(root_in, 9 + place, me_g), root_recv, (root, 0)).start()
+        send(j_out(3, 0), slot(root_in, 9 + place, me_g), root_recv.at[0], (root, 0)).start()
 
     give_i(3, [last_recv.at[0], last_recv.at[1]])
     give_j(3, 0, -1, last_recv.at[2])
@@ -544,7 +544,7 @@
 
     @pl.when(is_first & (me_g != root))
     def _():
-        send(j_out(3, 0), slot(root_in, 0, me_g), root_recv, (root, 0)).start()
+        send(j_out(3, 0), slot(root_in, 0, me_g), root_recv.at[0], (root, 0)).start()
 
     inside = assemble_inside(local, ez)
 
@@ -572,17 +572,17 @@
 
     @pl.when(is_mid)
     def _():
-        send(side_out.at[pl.ds(0, q)], slot(root_in, 10 + place, me_g), root_recv, (root, 0)).start()
+        send(side_out.at[pl.ds(0, q)], slot(root_in, 10 + place, me_g), root_recv.at[0], (root, 0)).start()
 
     @pl.when(is_first & (me_g != root))
     def _():
-        send(side_out.at[pl.ds(0, q)], slot(root_in, 1, me_g), root_recv, (root, 0)).start()
+        send(side_out.at[pl.ds(0, q)], slot(root_in, 1, me_g), root_recv.at[0], (root, 0)).start()
 
     @pl.when(is_near)
     def _():
         side_out[pl.ds(q, q)] = shared(1)
         dst = root_in.at[pl.ds(pl.multiple_of(q * (6 * ng + 2 * me_g), q), 2 * q)]
-        send(side_out.at[pl.ds(0, 2 * q)], dst, root_recv, (root, 0)).start()
+        send(side_out.at[pl.ds(0, 2 * q)], dst, root_recv.at[0], (root, 0)).start()
 
     dual = add_j_face(mixed, ez, *turns(2, 0), 1)
     norm_now = total_of([spread_res[b] * residual[b] * inverse[b] for b in range(4)])
@@ -667,7 +667,7 @@
     def _():
         slot(root_in, 0, me_g)[...] = j_out(3, 0)[...]
         slot(root_in, 1, me_g)[...] = side_out[pl.ds(0, q)]
-        drain((20 * ng - 2) * q + ng // 2 * h + ng * u, root_recv)
+        drain((19 * ng - 2) * q + ng // 2 * h, root_recv.at[0])
 
         def far(g):
             return wrap_in[pl.ds(u * g + (0 if g & 1 else h), q)]
@@ -687,18 +687,27 @@
         groups = range(ng)
         seams = (
             ([got(3, g) + got(4, g) for g in groups], [paired(g, 0) for g in groups]),
-            ([got(2, g) + got(5, g) for g in groups], [paired(g, 1) for g in groups]),
             ([got(8, g) + got(9, g) for g in groups], [got(10, g) for g in groups]),
             ([got(11, g) + got(12, g) for g in groups], [got(13, g) for g in groups]),
             ([got(14, g) + got(15, g) for g in groups], [got(16, g) for g in groups]),
             ([got(17, g) + got(18, g) for g in groups], [got(19, g) for g in groups]),
+        )
+
+        def add_seams(total, seams):
+            for faces, fits in seams:
+                for g in groups:
+                    face = faces[g] + jnp.where(seam, roll(faces[(g + 1) % ng], 88), 0.0)
+                    term = face * face * fits[g]
+                    total = term if total is None else total + term
+            return total
+
+        total = add_seams(total, seams)
+        drain(ng * (u + q), root_recv.at[1])
+        seams = (
+            ([got(2, g) + got(5, g) for g in groups], [paired(g, 1) for g in groups]),
             ([got(0, g) + far(g) for g in groups], [got(1, g) for g in groups]),
         )
-        for faces, fits in seams:
-            for g in groups:
-                face = faces[g] + jnp.where(seam, roll(faces[(g + 1) % ng], 88), 0.0)
-                term = face * face * fits[g]
-                total = term if total is None else total + term
+        total = add_seams(total, seams)
         for g in range(1, ng, 2):
             face = across(g) + across((g + 1) % ng)
             term = face * face * side_in[pl.ds(h * (g // 2), h)]
@@ -842,7 +851,7 @@
             pltpu.SemaphoreType.DMA,
             pltpu.SemaphoreType.DMA((2,)),
             pltpu.SemaphoreType.DMA((4,)),
-            pltpu.SemaphoreType.DMA,
+            pltpu.SemaphoreType.DMA((2,)),
             pltpu.SemaphoreType.DMA((3,)),
             pltpu.SemaphoreType.DMA,
             pltpu.SemaphoreType.DMA,

time: 17.2 us -> 17.2 us (level)
  no operation moved by 1% of the time
where the time goes in v8:
time: 17.2 us; the launch traced here: 17 us
  Pallas kernels  16.4 us (95%)
  between operations  0.64 us (4%)
    pallas_call x1, Pallas kernels, on_device(): pl.pallas_call(functools.partial(kernel, ng, nd, ez), out_shape=pltpu.VME...  15.7 us
    pallas_call x1, Pallas kernels, on_device(): pl.pallas_call(deliver, out_shape=[jax.ShapeDtypeStruct(flat, f32)] * 3,...  0.68 us

profile of v8, /device:TPU:0, one launch (start us, length us, event | category | flops | bytes accessed | tf_op | source)
XLA Modules:
  0.0 17.0 jit_solution(11629514121001567507)
XLA Ops:
  0.6 15.7 %shard_map.85.stacked = f32[3,32,512]{2,1,0:T(8,128)S(1)} custom-call(f32[32,512]{1,0:T(8,128)} %bitcast.9, f32[32,512]{1,0:T(8,128)} %bitcast.10, f32[32,512]{1,0:T(8,128)} %bitcast.11, bf16[3,32,512]{2,1,0:T(8,128)(2,1)} %bitcast.8, bf16[32,512]{1,0:T(8,128)(2,1)} %bitcast.12, bf16[256,1024]{1,0:T(8,128)(2,1)} %constant.2.clone.tab_h), custom_call_target="tpu_custom_call" | custom-call | tf_op jit(solution)/shard_map/pallas_call | solution.py:822
  16.3 0.7 %shard_map.86 = (f32[32,512]{1,0:T(8,128)}, f32[32,512]{1,0:T(8,128)}, f32[32,512]{1,0:T(8,128)}) custom-call(f32[3,32,512]{2,1,0:T(8,128)S(1)} %shard_map.85.stacked), custom_call_target="tpu_custom_call" | custom-call | tf_op jit(solution)/shard_map/pallas_call | solution.py:869
